TPU v7x, 32 devices: a whole 2x2x4 slice. The times are simulated.
32 devices in a mesh: data: 32 (over z, y, x, core).
Axes of the slice: x: 2, y: 2, z: 4, core: 2. Of those that a mesh axis runs over, the one named last changes fastest.
Arguments:
- x_in: bfloat16 [1024, 16, 256], P('data')
- targets: int32 [1024, 16], P('data')
- w_lstm: bfloat16 [8, 512, 1024], replicated
- b_lstm: float32 [8, 1024], replicated
- w_vocab: bfloat16 [256, 32000], replicated
Outputs:
- output 1: float32 [8, 512, 1024], replicated
- output 2: float32 [8, 1024], replicated
- output 3: float32 [256, 32000], replicated
- output 4: float32 [1024, 16, 256], P('data')
All inputs are finite; a program needn't handle non-finite values.
Results may differ from a plain program's by a relative error of at most 0.00384.
Values are sent between devices in bfloat16 or wider.
A program may use at most 1 GiB of HBM per device.

v0:
```python
import jax
import jax.numpy as jnp
from jax import lax
from jax.sharding import PartitionSpec as P


def lstm_forward(seq_in, w_layer, b_layer):
    seq_len, num_rows, hidden = seq_in.shape
    w_rec = w_layer[hidden:]
    z_in = jnp.einsum('tbk,kn->tbn', seq_in, w_layer[:hidden], preferred_element_type=jnp.float32) + b_layer

    def time_step(carry_in, z_step):
        h_low, c_prev = carry_in
        z_all = z_step + jnp.dot(h_low, w_rec, preferred_element_type=jnp.float32)
        gate_i = jax.nn.sigmoid(z_all[:, :hidden])
        gate_f = jax.nn.sigmoid(z_all[:, hidden:2 * hidden])
        gate_g = jnp.tanh(z_all[:, 2 * hidden:3 * hidden])
        gate_o = jax.nn.sigmoid(z_all[:, 3 * hidden:])
        c_new = gate_f * c_prev + gate_i * gate_g
        tanh_c = jnp.tanh(c_new)
        h_new = gate_o * tanh_c
        gate_all = jnp.concatenate([gate_i, gate_f, gate_g, gate_o], axis=-1)
        return (h_new.astype(jnp.bfloat16), c_new), (h_new, h_low, gate_all, c_prev, tanh_c)

    init_state = (jnp.zeros((num_rows, hidden), jnp.bfloat16), jnp.zeros((num_rows, hidden), jnp.float32))
    final_state, stored = lax.scan(time_step, init_state, z_in)
    h_seq, h_prev, gate_seq, c_prev_seq, tanh_seq = stored
    u_seq = jnp.concatenate([seq_in, h_prev], axis=-1)
    next_in = (seq_in.astype(jnp.float32) + h_seq).astype(jnp.bfloat16)
    return next_in, (u_seq, gate_seq, c_prev_seq, tanh_seq)


def lstm_backward(d_out, stored, w_layer):
    u_seq, gate_seq, c_prev_seq, tanh_seq = stored
    seq_len, num_rows, hidden = d_out.shape
    w_rec = w_layer[hidden:]

    def time_step(carry_in, step_in):
        dh_rec, dc_next = carry_in
        d_ext, gate_all, cell_prev, tanh_c = step_in
        gate_i = gate_all[:, :hidden]
        gate_f = gate_all[:, hidden:2 * hidden]
        gate_g = gate_all[:, 2 * hidden:3 * hidden]
        gate_o = gate_all[:, 3 * hidden:]
        grad_h = d_ext + dh_rec
        dc_tot = dc_next + grad_h * gate_o * (1.0 - tanh_c * tanh_c)
        dz_all = jnp.concatenate([
            dc_tot * gate_g * gate_i * (1.0 - gate_i),
            dc_tot * cell_prev * gate_f * (1.0 - gate_f),
            dc_tot * gate_i * (1.0 - gate_g * gate_g),
            grad_h * tanh_c * gate_o * (1.0 - gate_o)], axis=-1)
        dz_low = dz_all.astype(jnp.bfloat16)
        dh_prev = jnp.einsum('bn,kn->bk', dz_low, w_rec, preferred_element_type=jnp.float32)
        return (dh_prev, dc_tot * gate_f), (dz_low, jnp.sum(dz_all, axis=0))

    init_state = (jnp.zeros((num_rows, hidden), jnp.float32), jnp.zeros((num_rows, hidden), jnp.float32))
    final_state, outs_seq = lax.scan(time_step, init_state, (d_out, gate_seq, c_prev_seq, tanh_seq), reverse=True)
    dz_seq, db_steps = outs_seq
    dw_layer = jnp.einsum('tbk,tbn->kn', u_seq, dz_seq, preferred_element_type=jnp.float32)
    d_in = d_out + jnp.einsum('tbn,kn->tbk', dz_seq, w_layer[:hidden], preferred_element_type=jnp.float32)
    return dw_layer, jnp.sum(db_steps, axis=0), d_in


def head_backward(top_in, tgt_seq, w_vocab):
    logits = jnp.einsum('tbk,kv->tbv', top_in, w_vocab, preferred_element_type=jnp.float32)
    prob_all = jax.nn.softmax(logits, axis=-1)
    vocab_ids = lax.broadcasted_iota(jnp.int32, (1, 1, w_vocab.shape[1]), 2)
    d_logits = jnp.where(vocab_ids == tgt_seq[:, :, None], prob_all - 1.0, prob_all).astype(jnp.bfloat16)
    dw_vocab = jnp.einsum('tbk,tbv->kv', top_in, d_logits, preferred_element_type=jnp.float32)
    d_top = jnp.einsum('tbv,kv->tbk', d_logits, w_vocab, preferred_element_type=jnp.float32)
    return d_top, dw_vocab


def solution(mesh):
    def local_grads(x_rows, tgt_rows, w_lstm, b_lstm, w_vocab):
        num_layers = w_lstm.shape[0]
        seq_in = jnp.swapaxes(x_rows, 0, 1)
        saved_acts = []
        for layer_idx in range(num_layers):
            seq_in, stored = lstm_forward(seq_in, w_lstm[layer_idx], b_lstm[layer_idx])
            saved_acts.append(stored)
        d_seq, dw_vocab = head_backward(seq_in, jnp.swapaxes(tgt_rows, 0, 1), w_vocab)
        dw_vocab = lax.psum(dw_vocab, 'data')
        dw_list = []
        db_list = []
        for layer_idx in reversed(range(num_layers)):
            dw_layer, db_layer, d_seq = lstm_backward(d_seq, saved_acts[layer_idx], w_lstm[layer_idx])
            dw_layer, db_layer = lax.psum((dw_layer, db_layer), 'data')
            dw_list.insert(0, dw_layer)
            db_list.insert(0, db_layer)
        return jnp.stack(dw_list), jnp.stack(db_list), dw_vocab, jnp.swapaxes(d_seq, 0, 1)

    return jax.shard_map(local_grads, mesh=mesh, in_specs=(P('data'), P('data'), P(), P(), P()), out_specs=(P(), P(), P(), P('data')), check_vma=False)
```

profile of v0, /device:TPU:0, one launch (start us, length us, event | category | flops | bytes accessed | tf_op | source)
XLA Modules:
  0.0 1810.9 jit_solution(12303649891571513932)
XLA Ops:
  7.5 3.6 slice_bitcast_fusion
  11.7 2.8 convolution_add_fusion.15
  19.4 80.1 %while.352 = (s32[]{:T(128)}, bf16[32,256]{1,0:T(8,128)(2,1)}, f32[32,256]{1,0:T(8,128)S(1)}, f32[16,32,256]{2,1,0:T(8,128)}, bf16[16,32,256]{2,1,0:T(8,128)(2,1...) while((s32[]{:T(128)}, bf16[32,256]{1,0:T(8,128)(2,1)}, ...), condition=%wide.region_1.2_spmd.clone, body=%wide.region_0.1_spmd.clone.sunk | while | flops 17129476 | bytes 1738885 | solution.py:26
  100.9 2.9 convolution_add_fusion.14
  108.0 50.0 %while.353 = (s32[]{:T(128)}, bf16[32,256]{1,0:T(8,128)(2,1)S(1)}, f32[32,256]{1,0:T(8,128)S(1)}, f32[16,32,256]{2,1,0:T(8,128)}, bf16[16,32,256]{2,1,0:T(8,128)...) while((s32[]{:T(128)}, bf16[32,256]{1,0:T(8,128)(2,1)S(1)}, ...), condition=%wide.region_3.4_spmd.clone, body=%wide.region_2.3_spmd.clone.sunk | while | flops 17129476 | bytes 1738377 | solution.py:26
  160.1 2.9 convolution_add_fusion.13
  166.4 49.9 %while.354 = (s32[]{:T(128)}, bf16[32,256]{1,0:T(8,128)(2,1)S(1)}, f32[32,256]{1,0:T(8,128)S(1)}, f32[16,32,256]{2,1,0:T(8,128)}, bf16[16,32,256]{2,1,0:T(8,128)...) while((s32[]{:T(128)}, bf16[32,256]{1,0:T(8,128)(2,1)S(1)}, ...), condition=%wide.region_5.6_spmd.clone, body=%wide.region_4.5_spmd.clone.sunk | while | flops 17129476 | bytes 1738377 | solution.py:26
  218.6 2.9 convolution_add_fusion.12
  224.8 40.5 %while.355 = (s32[]{:T(128)}, bf16[32,256]{1,0:T(8,128)(2,1)S(1)}, f32[32,256]{1,0:T(8,128)S(1)}, f32[16,32,256]{2,1,0:T(8,128)S(1)}, bf16[16,32,256]{2,1,0:T(8,...) while((s32[]{:T(128)}, bf16[32,256]{1,0:T(8,128)(2,1)S(1)}, ...), condition=%wide.region_7.8_spmd.clone, body=%wide.region_6.7_spmd.clone.sunk | while | flops 17129476 | bytes 1737869 | solution.py:26
  265.5 3.1 convolution_add_fusion.11
  271.2 40.6 %while.356 = (s32[]{:T(128)}, bf16[32,256]{1,0:T(8,128)(2,1)S(1)}, f32[32,256]{1,0:T(8,128)S(1)}, f32[16,32,256]{2,1,0:T(8,128)S(1)}, bf16[16,32,256]{2,1,0:T(8,...) while((s32[]{:T(128)}, bf16[32,256]{1,0:T(8,128)(2,1)S(1)}, ...), condition=%wide.region_9.10_spmd.clone, body=%wide.region_8.9_spmd.clone.sunk | while | flops 17129476 | bytes 1737869 | solution.py:26
  312.7 3.2 convolution_add_fusion.10
  317.6 30.9 %while.357 = (s32[]{:T(128)}, bf16[32,256]{1,0:T(8,128)(2,1)S(1)}, f32[32,256]{1,0:T(8,128)S(1)}, f32[16,32,256]{2,1,0:T(8,128)S(1)}, bf16[16,32,256]{2,1,0:T(8,...) while((s32[]{:T(128)}, bf16[32,256]{1,0:T(8,128)(2,1)S(1)}, ...), condition=%wide.region_11.12_spmd.clone, body=%wide.region_10.11_spmd.clone.sunk | while | flops 17129476 | bytes 1737361 | solution.py:26
  349.5 3.2 convolution_add_fusion.9
  354.5 31.0 %while.358 = (s32[]{:T(128)}, bf16[32,256]{1,0:T(8,128)(2,1)S(1)}, f32[32,256]{1,0:T(8,128)S(1)}, f32[16,32,256]{2,1,0:T(8,128)S(1)}, bf16[16,32,256]{2,1,0:T(8,...) while((s32[]{:T(128)}, bf16[32,256]{1,0:T(8,128)(2,1)S(1)}, ...), condition=%wide.region_13.14_spmd.clone, body=%wide.region_12.13_spmd.clone.sunk | while | flops 17129476 | bytes 1737361 | solution.py:26
  385.7 3.1 convolution_add_fusion.8
  390.6 31.0 %while.359 = (s32[]{:T(128)}, bf16[32,256]{1,0:T(8,128)(2,1)S(1)}, f32[32,256]{1,0:T(8,128)S(1)}, f32[16,32,256]{2,1,0:T(8,128)S(1)}, bf16[16,32,256]{2,1,0:T(8,...) while((s32[]{:T(128)}, bf16[32,256]{1,0:T(8,128)(2,1)S(1)}, ...), condition=%wide.region_15.16_spmd.clone, body=%wide.region_14.15_spmd.clone.sunk | while | flops 17129476 | bytes 1737361 | solution.py:26
  421.6 28.7 %fusion.296 = (f32[16,32]{1,0:T(8,128)S(1)}, f32[16,32,32000]{2,1,0:T(8,128)}) fusion(bf16[256,32000]{1,0:T(8,128)(2,1)} %param.41, f32[16,32,256]{2,1,0:T(8,128)S(1)} %get-tuple-element.2052, bf16[16,32,256]{2,1,0:T(8,128)(2,1)S(1)} %add_convert_fusion.1), kind=kOutput, calls=%fused_computation.533 | convolution fusion | flops 8405384704 | bytes 82708480 | tf_op jit(solution)/shard_map/tbk,kv->tbv/dot_general | solution.py:65
  450.4 20.8 %fusion.201 = f32[16,32]{1,0:T(8,128)S(1)} fusion(f32[16,32,32000]{2,1,0:T(8,128)} %get-tuple-element.3170, f32[16,32]{1,0:T(8,128)S(1)} %get-tuple-element.3169), kind=kLoop, calls=%fused_computation.412 | loop fusion | flops 32767488 | bytes 65540096 | tf_op jit(solution)/shard_map/reduce_sum | solution.py:66
  471.2 32.9 %fusion.200 = bf16[16,32,32000]{2,1,0:T(8,128)(2,1)} fusion(f32[16,32,32000]{2,1,0:T(8,128)} %get-tuple-element.3170, f32[16,32]{1,0:T(8,128)S(1)} %fusion.201, f32[16,32]{1,0:T(8,128)S(1)} %get-tuple-element.3169, s32[16,32]{1,0:T(8,128)S(1)} %bitcast.804), kind=kLoop, calls=%fused_computation.409 | loop fusion | flops 98304000 | bytes 98310144 | tf_op jit(solution)/shard_map/convert_element_type | solution.py:68
  504.0 19.0 %fusion.202 = f32[16,32,256]{2,1,0:T(8,128)} fusion(bf16[16,32,32000]{2,1,0:T(8,128)(2,1)} %fusion.200, bf16[256,32000]{1,0:T(8,128)(2,1)} %param.41), kind=kOutput, calls=%fused_computation.414 | convolution fusion | flops 8388608000 | bytes 49676288 | tf_op jit(solution)/shard_map/tbv,kv->tbk/dot_general | solution.py:70
  523.1 27.4 %convolution_bitcast_fusion = f32[256,32000]{1,0:T(8,128)} fusion(bf16[16,32,32000]{2,1,0:T(8,128)(2,1)} %fusion.200, f32[16,32,256]{2,1,0:T(8,128)S(1)} %get-tuple-element.2052, bf16[16,32,256]{2,1,0:T(8,128)(2,1)S(1)} %add_convert_fusion.1), kind=kOutput, calls=%fused_computation.413 | convolution fusion | flops 8389001216 | bytes 66322432 | tf_op jit(solution)/shard_map/tbk,tbv->kv/dot_general | solution.py:69
  551.4 47.2 %while.360 = (s32[]{:T(128)}, f32[32,256]{1,0:T(8,128)S(1)}, f32[32,256]{1,0:T(8,128)S(1)}, bf16[16,32,1024]{2,1,0:T(8,128)(2,1)S(1)}, f32[16,1024]{1,0:T(8,128)...) while((s32[]{:T(128)}, f32[32,256]{1,0:T(8,128)S(1)}, ...), condition=%wide.region_20.21_spmd.clone, body=%wide.region_18.20_spmd.clone.sunk | while | flops 17660932 | bytes 1880231 | solution.py:57
  601.9 67.6 %while.361 = (s32[]{:T(128)}, f32[32,256]{1,0:T(8,128)S(1)}, f32[32,256]{1,0:T(8,128)S(1)}, bf16[16,32,1024]{2,1,0:T(8,128)(2,1)S(1)}, f32[16,1024]{1,0:T(8,128)...) while((s32[]{:T(128)}, f32[32,256]{1,0:T(8,128)S(1)}, ...), condition=%wide.region_23.24_spmd.clone, body=%wide.region_21.23_spmd.clone.sunk | while | flops 17660932 | bytes 1880231 | solution.py:57
  669.6 2.9 convolution_add_fusion.22
  673.6 57.0 %while.362 = (s32[]{:T(128)}, f32[32,256]{1,0:T(8,128)S(1)}, f32[32,256]{1,0:T(8,128)S(1)}, bf16[16,32,1024]{2,1,0:T(8,128)(2,1)}, f32[16,1024]{1,0:T(8,128)S(1)...) while((s32[]{:T(128)}, f32[32,256]{1,0:T(8,128)S(1)}, ...), condition=%wide.region_26.27_spmd.clone, body=%wide.region_24.26_spmd.clone.sunk | while | flops 17660932 | bytes 1880231 | solution.py:57
  730.6 2.8 convolution_add_fusion.21
  733.7 47.2 %while.363 = (s32[]{:T(128)}, f32[32,256]{1,0:T(8,128)S(1)}, f32[32,256]{1,0:T(8,128)S(1)}, bf16[16,32,1024]{2,1,0:T(8,128)(2,1)S(1)}, f32[16,1024]{1,0:T(8,128)...) while((s32[]{:T(128)}, f32[32,256]{1,0:T(8,128)S(1)}, ...), condition=%wide.region_29.30_spmd.clone, body=%wide.region_27.29_spmd.clone.sunk | while | flops 17660932 | bytes 1880231 | solution.py:57
  780.9 2.9 convolution_add_fusion.20
  785.0 57.1 %while.364 = (s32[]{:T(128)}, f32[32,256]{1,0:T(8,128)S(1)}, f32[32,256]{1,0:T(8,128)S(1)}, bf16[16,32,1024]{2,1,0:T(8,128)(2,1)}, f32[16,1024]{1,0:T(8,128)S(1)...) while((s32[]{:T(128)}, f32[32,256]{1,0:T(8,128)S(1)}, ...), condition=%wide.region_32.33_spmd.clone, body=%wide.region_30.32_spmd.clone.sunk | while | flops 17660932 | bytes 1880231 | solution.py:57
  842.1 2.8 convolution_add_fusion.19
  845.1 47.2 %while.365 = (s32[]{:T(128)}, f32[32,256]{1,0:T(8,128)S(1)}, f32[32,256]{1,0:T(8,128)S(1)}, bf16[16,32,1024]{2,1,0:T(8,128)(2,1)S(1)}, f32[16,1024]{1,0:T(8,128)...) while((s32[]{:T(128)}, f32[32,256]{1,0:T(8,128)S(1)}, ...), condition=%wide.region_35.36_spmd.clone, body=%wide.region_33.35_spmd.clone.sunk | while | flops 17660932 | bytes 1880231 | solution.py:57
  892.4 2.9 convolution_add_fusion.18
  896.4 57.1 %while.366 = (s32[]{:T(128)}, f32[32,256]{1,0:T(8,128)S(1)}, f32[32,256]{1,0:T(8,128)S(1)}, bf16[16,32,1024]{2,1,0:T(8,128)(2,1)}, f32[16,1024]{1,0:T(8,128)S(1)...) while((s32[]{:T(128)}, f32[32,256]{1,0:T(8,128)S(1)}, ...), condition=%wide.region_38.39_spmd.clone, body=%wide.region_36.38_spmd.clone.sunk | while | flops 17660932 | bytes 1880231 | solution.py:57
  953.5 2.8 convolution_add_fusion.17
  957.1 67.7 %while.367 = (s32[]{:T(128)}, f32[32,256]{1,0:T(8,128)S(1)}, f32[32,256]{1,0:T(8,128)S(1)}, bf16[16,32,1024]{2,1,0:T(8,128)(2,1)S(1)}, f32[16,1024]{1,0:T(8,128)...) while((s32[]{:T(128)}, f32[32,256]{1,0:T(8,128)S(1)}, ...), condition=%wide.region_41.42_spmd.clone, body=%wide.region_39.41_spmd.clone.sunk | while | flops 17660932 | bytes 1880231 | solution.py:57
  1024.9 3.2 convolution_bitcast_fusion.1
  1047.5 43.7 %all-reduce = (f32[1,1024]{1,0:T(1,128)S(1)}, f32[1,1024]{1,0:T(1,128)S(1)}, f32[1,1024]{1,0:T(1,128)S(1)}, f32[1,1024]{1,0:T(1,128)S(1)}, f32[1,1024]{1,0:T(1,1...) all-reduce(f32[1,1024]{1,0:T(1,128)S(1)} %bitcast.796, ...), channel_id=1, replica_groups=mesh['data'=32] {'data'}, use_global_device_ids=true, to_apply=%region_51.52 | all-reduce | flops 8192 | bytes 65536 | tf_op jit(solution)/shard_map/psum | solution.py:88
  1091.9 673.1 %all-reduce.4.cloned.1.call-done = (f32[1,512,1024]{2,1,0:T(8,128)}, f32[1,512,1024]{2,1,0:T(8,128)}, f32[1,512,1024]{2,1,0:T(8,128)}, f32[1,512,1024]{2,1,0:T(8...) async-done(((f32[1,512,1024]{2,1,0:T(8,128)}, ...) | async-done | bytes 49545232 | tf_op jit(solution)/shard_map/psum | solution.py:88
  1765.0 3.3 constant_dynamic-update-slice_fusion.7
  1768.3 3.9 constant_dynamic-update-slice_fusion.6
  1772.2 3.9 constant_dynamic-update-slice_fusion.5
  1776.1 3.9 constant_dynamic-update-slice_fusion.4
  1780.0 3.2 constant_dynamic-update-slice_fusion.3
  1783.2 3.2 constant_dynamic-update-slice_fusion.2
  1786.3 3.2 constant_dynamic-update-slice_fusion.1
  1789.5 3.2 constant_dynamic-update-slice_fusion
  1792.6 11.4 copy.408
  (1960 shorter events, 855.4 us)
Async XLA Ops:
  7.2 1757.8 %all-reduce.4.cloned.1.call-start = ((), (), s32[]{:S(2)}) async-start(), calls=%async_computation | async-start | bytes 99090432 | tf_op jit(solution)/shard_map/psum | solution.py:88
  7.4 4.2 copy-start.25
  99.5 5.9 copy-start
  100.9 4.5 copy-start.27
  108.0 50.8 %copy-start.28 = (bf16[16,32,256]{2,1,0:T(8,128)(2,1)S(1)}, bf16[16,32,256]{2,1,0:T(8,128)(2,1)}, u32[]{:S(2)}) copy-start(bf16[16,32,256]{2,1,0:T(8,128)(2,1)} %copy-done.27) | copy-start | bytes 786436
  158.7 5.8 copy-start.2
  160.1 57.1 %copy-start.30 = (bf16[16,32,256]{2,1,0:T(8,128)(2,1)}, bf16[16,32,256]{2,1,0:T(8,128)(2,1)S(1)}, u32[]{:S(2)}) copy-start(bf16[16,32,256]{2,1,0:T(8,128)(2,1)S(1)} %add_convert_fusion.6) | copy-start | bytes 786436
  166.4 52.2 %copy-start.87 = (f32[1,1024]{1,0:T(1,128)S(1)}, f32[1,1024]{1,0:T(1,128)}, u32[]{:S(2)}) copy-start(f32[1,1024]{1,0:T(1,128)} %get-tuple-element.3164) | copy-start | bytes 12292
  217.1 4.3 copy-start.60
  217.1 5.9 copy-start.4
  218.5 46.9 %copy-start.32 = (bf16[16,32,256]{2,1,0:T(8,128)(2,1)}, bf16[16,32,256]{2,1,0:T(8,128)(2,1)S(1)}, u32[]{:S(2)}) copy-start(bf16[16,32,256]{2,1,0:T(8,128)(2,1)S(1)} %add_convert_fusion.5) | copy-start | bytes 786436
  224.8 40.7 %copy-start.86 = (f32[1,1024]{1,0:T(1,128)S(1)}, f32[1,1024]{1,0:T(1,128)}, u32[]{:S(2)}) copy-start(f32[1,1024]{1,0:T(1,128)} %get-tuple-element.3163) | copy-start | bytes 12292
  265.4 4.9 copy-start.6
  265.4 4.9 copy-start.62
  265.5 47.1 %copy-start.34 = (bf16[16,32,256]{2,1,0:T(8,128)(2,1)}, bf16[16,32,256]{2,1,0:T(8,128)(2,1)S(1)}, u32[]{:S(2)}) copy-start(bf16[16,32,256]{2,1,0:T(8,128)(2,1)S(1)} %add_convert_fusion.4) | copy-start | bytes 786436
  271.2 41.4 %copy-start.85 = (f32[1,1024]{1,0:T(1,128)S(1)}, f32[1,1024]{1,0:T(1,128)}, u32[]{:S(2)}) copy-start(f32[1,1024]{1,0:T(1,128)} %get-tuple-element.3162) | copy-start | bytes 12292
  312.6 4.8 copy-start.8
  312.6 4.8 copy-start.41
  312.6 36.7 %copy-start.36 = (bf16[16,32,256]{2,1,0:T(8,128)(2,1)}, bf16[16,32,256]{2,1,0:T(8,128)(2,1)S(1)}, u32[]{:S(2)}) copy-start(bf16[16,32,256]{2,1,0:T(8,128)(2,1)S(1)} %add_convert_fusion.3) | copy-start | bytes 786436
  317.6 31.9 %copy-start.84 = (f32[1,1024]{1,0:T(1,128)S(1)}, f32[1,1024]{1,0:T(1,128)}, u32[]{:S(2)}) copy-start(f32[1,1024]{1,0:T(1,128)} %get-tuple-element.3168) | copy-start | bytes 12292
  349.3 5.0 copy-start.10
  349.4 5.0 copy-start.45
  349.4 5.0 copy-start.66
  349.4 36.1 %copy-start.38 = (bf16[16,32,256]{2,1,0:T(8,128)(2,1)}, bf16[16,32,256]{2,1,0:T(8,128)(2,1)S(1)}, u32[]{:S(2)}) copy-start(bf16[16,32,256]{2,1,0:T(8,128)(2,1)S(1)} %add_convert_fusion.2) | copy-start | bytes 786436
  354.5 31.2 %copy-start.83 = (f32[1,1024]{1,0:T(1,128)S(1)}, f32[1,1024]{1,0:T(1,128)}, u32[]{:S(2)}) copy-start(f32[1,1024]{1,0:T(1,128)} %get-tuple-element.3161) | copy-start | bytes 12292
  385.5 4.9 copy-start.43
  385.5 4.9 copy-start.46
  385.6 4.8 copy-start.68
  421.6 28.8 %copy-start.44 = (f32[16,32,256]{2,1,0:T(8,128)}, f32[16,32,256]{2,1,0:T(8,128)S(1)}, u32[]{:S(2)}) copy-start(f32[16,32,256]{2,1,0:T(8,128)S(1)} %get-tuple-element.4731) | copy-start | bytes 1572868
  421.6 28.8 %copy-start.47 = (f32[16,32,256]{2,1,0:T(8,128)}, f32[16,32,256]{2,1,0:T(8,128)S(1)}, u32[]{:S(2)}) copy-start(f32[16,32,256]{2,1,0:T(8,128)S(1)} %get-tuple-element.4730) | copy-start | bytes 1572868
  421.6 28.7 %copy-start.70 = (bf16[16,32,256]{2,1,0:T(8,128)(2,1)}, bf16[16,32,256]{2,1,0:T(8,128)(2,1)S(1)}, u32[]{:S(2)}) copy-start(bf16[16,32,256]{2,1,0:T(8,128)(2,1)S(1)} %get-tuple-element.2091) | copy-start | bytes 786436
  450.4 20.8 %copy-start.88 = (s32[32,16]{0,1:T(8,128)S(1)}, s32[32,16]{0,1:T(8,128)}, u32[]{:S(2)}) copy-start(s32[32,16]{0,1:T(8,128)} %param.38) | copy-start | bytes 6148
  523.1 27.4 %copy-start.26 = (bf16[32,16,256]{2,1,0:T(8,128)(2,1)S(1)}, bf16[32,16,256]{2,1,0:T(8,128)(2,1)}, u32[]{:S(2)}) copy-start(bf16[32,16,256]{2,1,0:T(8,128)(2,1)} %param.37) | copy-start | bytes 786436
  523.1 28.4 %copy-start.55 = (f32[32,256]{1,0:T(8,128)S(1)}, f32[32,256]{1,0:T(8,128)}, u32[]{:S(2)}) copy-start(f32[32,256]{1,0:T(8,128)} %custom-call.16) | copy-start | bytes 98308
  669.5 4.0 copy-start.15
  669.5 4.0 copy-start.11
  669.6 4.0 copy-start.53
  780.9 4.1 copy-start.18
  780.9 4.1 copy-start.73
  780.9 4.0 copy-start.7
  780.9 4.0 copy-start.51
  892.3 4.1 copy-start.21
  892.3 4.1 copy-start.77
  892.3 4.0 copy-start.3
  892.4 4.0 copy-start.49
  953.5 3.7 copy-start.79
  953.5 3.6 copy-start.1
  1765.0 27.7 %copy-start.14 = (f32[256,32000]{1,0:T(8,128)S(1)}, f32[256,32000]{1,0:T(8,128)}, u32[]{:S(2)}) copy-start(f32[256,32000]{1,0:T(8,128)} %get-tuple-element.5037) | copy-start | bytes 98304000
  (42 other events, 97.9 us)
Sparse Core Ops, SparseCore 0:
  1042.8 722.0 all-reduce.3
where the time goes:
time: 1840 us; the launch traced here: 1810 us
  waiting for transfers between devices  673 us (37%)
  other arithmetic  506 us (28%)
  matrix products  311 us (17%)
  local copies, waits for them, and re-layouts  254 us (14%)
  blocking collectives  43.7 us (2%)
    psum x1, waiting for transfers between devices, local_grads(): dw_layer, db_layer = lax.psum((dw_layer, db_layer), 'data')  673 us
    concatenate x256, other arithmetic, time_step(): jnp.concatenate([dc_tot * gate_g * gate_i * (1.0 - gate_i), dc_tot * cell...  203 us
    dynamic_update_slice x512, other arithmetic, lstm_forward(): final_state, stored = lax.scan(time_step, init_state, z_in)  194 us
    dot_general x128, matrix products, time_step(): z_all = z_step + jnp.dot(h_low, w_rec, preferred_element_type=jnp.float32)  141 us
    squeeze x128, local copies, waits for them, and re-layouts, lstm_forward(): final_state, stored = lax.scan(time_step, init_state, z_in)  120 us
    dynamic_update_slice x128, local copies, waits for them, and re-layouts, lstm_backward(): lax.scan(time_step, init_state, (d_out, gate_seq, c_prev_seq, tanh_seq),...  55.2 us
    psum x1, blocking collectives, local_grads(): dw_layer, db_layer = lax.psum((dw_layer, db_layer), 'data')  43.7 us
    unnamed x188, local copies, waits for them, and re-layouts  42.3 us
  transfers between devices with their start and end apart: 1, of which 1 were waited for; matrix products, arithmetic and copies ran while one was open for 0% of the time, Pallas kernels for 0%

commit v1 on v0

v1 whole, which is shorter than its diff:
```python
import functools

import jax
import jax.numpy as jnp
from jax import lax
from jax.experimental import pallas as pl
from jax.experimental.pallas import tpu as pltpu
from jax.sharding import PartitionSpec as P

F32 = jnp.float32
BF16 = jnp.bfloat16
VMEM_CAP = 60 * 1024 * 1024
VOCAB_BLK = 1280
SHARD = 1024


def mm(lhs, rhs, dims=((1,), (0,))):
    return lax.dot_general(lhs, rhs, (dims, ((), ())), preferred_element_type=F32)


def sig(val):
    return 0.5 * jnp.tanh(0.5 * val) + 0.5


def fwd_kernel(steps, rows, hid, x_ref, w_ref, b_ref, u_ref, coef_ref, top_ref, xs, zin):
    layer = pl.program_id(0)

    @pl.when(layer == 0)
    def _():
        xs[...] = x_ref[...]

    x_val = xs[...]
    u_ref[0, :, :hid] = x_val
    zin[...] = mm(x_val, w_ref[0, :hid, :]) + b_ref[0]
    h_low = jnp.zeros((rows, hid), BF16)
    cell = jnp.zeros((rows, hid), F32)
    for step in range(steps):
        ts = pl.ds(step * rows, rows)
        u_ref[0, ts, hid:] = h_low
        z_all = zin[ts, :]
        if step:
            z_all = z_all + mm(h_low, w_ref[0, hid:, :])
        gi = sig(z_all[:, :hid])
        gf = sig(z_all[:, hid:2 * hid])
        gg = jnp.tanh(z_all[:, 2 * hid:3 * hid])
        go = sig(z_all[:, 3 * hid:])
        c_new = gf * cell + gi * gg
        tc = jnp.tanh(c_new)
        h_new = go * tc
        h_low = h_new.astype(BF16)
        coef_ref[0, ts, 0 * hid:1 * hid] = gg * gi * (1.0 - gi)
        coef_ref[0, ts, 1 * hid:2 * hid] = cell * gf * (1.0 - gf)
        coef_ref[0, ts, 2 * hid:3 * hid] = gi * (1.0 - gg * gg)
        coef_ref[0, ts, 3 * hid:4 * hid] = tc * go * (1.0 - go)
        coef_ref[0, ts, 4 * hid:5 * hid] = go * (1.0 - tc * tc)
        coef_ref[0, ts, 5 * hid:6 * hid] = gf
        cell = c_new
        xs[ts, :] = (xs[ts, :].astype(F32) + h_new).astype(BF16)

    @pl.when(layer == pl.num_programs(0) - 1)
    def _():
        top_ref[...] = xs[...]


def run_fwd(x_tok, w_lstm, b_lstm, steps, rows):
    layers, _, wide = w_lstm.shape
    hid = wide // 4
    tok = steps * rows
    return pl.pallas_call(
        functools.partial(fwd_kernel, steps, rows, hid),
        grid=(layers,),
        in_specs=[
            pl.BlockSpec((tok, hid), lambda i: (0, 0)),
            pl.BlockSpec((1, 2 * hid, wide), lambda i: (i, 0, 0)),
            pl.BlockSpec((1, 1, wide), lambda i: (i, 0, 0)),
        ],
        out_specs=[
            pl.BlockSpec((1, tok, 2 * hid), lambda i: (i, 0, 0)),
            pl.BlockSpec((1, tok, 6 * hid), lambda i: (i, 0, 0)),
            pl.BlockSpec((tok, hid), lambda i: (0, 0)),
        ],
        out_shape=[
            jax.ShapeDtypeStruct((layers, tok, 2 * hid), BF16),
            jax.ShapeDtypeStruct((layers, tok, 6 * hid), F32),
            jax.ShapeDtypeStruct((tok, hid), BF16),
        ],
        scratch_shapes=[pltpu.VMEM((tok, hid), BF16), pltpu.VMEM((tok, wide), F32)],
        compiler_params=pltpu.CompilerParams(vmem_limit_bytes=VMEM_CAP),
        name='lstm_fwd',
        cost_estimate=pl.CostEstimate(flops=70_000_000_000, bytes_accessed=40_000_000, transcendentals=0),
    )(x_tok, w_lstm, b_lstm.reshape(layers, 1, wide))


def head_kernel(blk, x_ref, w_ref, tgt_ref, dtop_ref, stat_ref, m_s, s_s, acc):
    phase, blk_id = pl.program_id(0), pl.program_id(1)
    tok = x_ref.shape[0]
    lanes = 128
    parts = blk // lanes
    chunk = 128

    @pl.when((phase == 0) & (blk_id == 0))
    def _():
        m_s[...] = jnp.full(m_s.shape, -jnp.inf, F32)
        s_s[...] = jnp.zeros(s_s.shape, F32)
        acc[...] = jnp.zeros(acc.shape, F32)

    @pl.when(phase == 0)
    def _():
        for r0 in range(0, tok, chunk):
            rs = pl.ds(r0, chunk)
            logits = mm(x_ref[rs, :], w_ref[...])
            cols = [logits[:, k * lanes:(k + 1) * lanes] for k in range(parts)]
            m_old = m_s[rs, :]
            m_new = functools.reduce(jnp.maximum, cols, m_old)
            tot = s_s[rs, :] * jnp.exp(m_old - m_new)
            for col in cols:
                tot = tot + jnp.exp(col - m_new)
            m_s[rs, :] = m_new
            s_s[rs, :] = tot

    @pl.when((phase == 0) & (blk_id == pl.num_programs(1) - 1))
    def _():
        m_lane = m_s[...]
        m_row = jnp.max(m_lane, axis=1, keepdims=True)
        s_row = jnp.sum(s_s[...] * jnp.exp(m_lane - m_row), axis=1, keepdims=True)
        m_rep = jnp.broadcast_to(m_row, m_lane.shape)
        r_rep = jnp.broadcast_to(1.0 / s_row, m_lane.shape)
        m_s[...] = m_rep
        s_s[...] = r_rep
        stat_ref[0:1, :] = m_rep.T[0:1, :]
        stat_ref[1:2, :] = r_rep.T[0:1, :]
        stat_ref[2:3, :] = tgt_ref[...].astype(F32).T[0:1, :]
        stat_ref[3:8, :] = jnp.zeros((5, tok), F32)

    @pl.when(phase == 1)
    def _():
        lane_id = lax.broadcasted_iota(jnp.int32, (chunk, lanes), 1) + blk_id * blk
        for r0 in range(0, tok, chunk):
            rs = pl.ds(r0, chunk)
            logits = mm(x_ref[rs, :], w_ref[...])
            m_row, r_row = m_s[rs, :], s_s[rs, :]
            off = tgt_ref[rs, :] - lane_id
            pieces = []
            for k in range(parts):
                prob = jnp.exp(logits[:, k * lanes:(k + 1) * lanes] - m_row) * r_row
                pieces.append(jnp.where(off == k * lanes, prob - 1.0, prob).astype(BF16))
            grad = jnp.concatenate(pieces, axis=1)
            acc[rs, :] += mm(grad, w_ref[...], ((1,), (1,)))

    @pl.when((phase == 1) & (blk_id == pl.num_programs(1) - 1))
    def _():
        dtop_ref[...] = acc[...]


def run_head(x_top, w_vocab, tgt_rep):
    tok, hid = x_top.shape
    vocab = w_vocab.shape[1]
    return pl.pallas_call(
        functools.partial(head_kernel, VOCAB_BLK),
        grid=(2, vocab // VOCAB_BLK),
        in_specs=[
            pl.BlockSpec((tok, hid), lambda p, j: (0, 0)),
            pl.BlockSpec((hid, VOCAB_BLK), lambda p, j: (0, j)),
            pl.BlockSpec((tok, 128), lambda p, j: (0, 0)),
        ],
        out_specs=[
            pl.BlockSpec((tok, hid), lambda p, j: (0, 0)),
            pl.BlockSpec((8, tok), lambda p, j: (0, 0)),
        ],
        out_shape=[jax.ShapeDtypeStruct((tok, hid), F32), jax.ShapeDtypeStruct((8, tok), F32)],
        scratch_shapes=[pltpu.VMEM((tok, 128), F32), pltpu.VMEM((tok, 128), F32), pltpu.VMEM((tok, hid), F32)],
        compiler_params=pltpu.CompilerParams(vmem_limit_bytes=VMEM_CAP),
        name='head',
        cost_estimate=pl.CostEstimate(flops=70_000_000_000, bytes_accessed=33_000_000, transcendentals=0),
    )(x_top, w_vocab, tgt_rep)


def vocab_kernel(start_ref, x_ref, stat_ref, w_ref, dw_ref, wt, acc):
    blk_id = pl.program_id(0)
    tok = x_ref.shape[0]
    shard = w_ref.shape[1]
    per = stat_ref.shape[0]
    chunk = 256

    @pl.when(blk_id == 0)
    def _():
        wt[...] = w_ref[...].T
        acc[...] = jnp.zeros(acc.shape, F32)

    stats = [jnp.concatenate([stat_ref[p, r:r + 1, :] for p in range(per)], axis=1) for r in range(3)]
    m_row, r_row = stats[0], stats[1]
    tgt = stats[2].astype(jnp.int32) - start_ref[0]
    x_val = x_ref[...]
    for r0 in range(0, shard, chunk):
        rs = pl.ds(r0, chunk)
        logits = mm(wt[rs, :], x_val, ((1,), (1,)))
        prob = jnp.exp(logits - m_row) * r_row
        ids = lax.broadcasted_iota(jnp.int32, (chunk, tok), 0) + r0
        grad = jnp.where(ids == tgt, prob - 1.0, prob).astype(BF16)
        acc[rs, :] += mm(grad, x_val)

    @pl.when(blk_id == pl.num_programs(0) - 1)
    def _():
        dw_ref[...] = acc[...].T


def run_vocab(start, x_all, stat_all, w_shard):
    tok, hid = x_all.shape
    ndev, _, per_dev = stat_all.shape
    per = 2
    shard = w_shard.shape[1]
    return pl.pallas_call(
        vocab_kernel,
        grid=(ndev // per,),
        in_specs=[
            pl.BlockSpec(memory_space=pltpu.SMEM),
            pl.BlockSpec((per * per_dev, hid), lambda i: (i, 0)),
            pl.BlockSpec((per, 8, per_dev), lambda i: (i, 0, 0)),
            pl.BlockSpec((hid, shard), lambda i: (0, 0)),
        ],
        out_specs=pl.BlockSpec((hid, shard), lambda i: (0, 0)),
        out_shape=jax.ShapeDtypeStruct((hid, shard), F32),
        scratch_shapes=[pltpu.VMEM((shard, hid), BF16), pltpu.VMEM((shard, hid), F32)],
        compiler_params=pltpu.CompilerParams(vmem_limit_bytes=VMEM_CAP),
        name='dw_vocab',
        cost_estimate=pl.CostEstimate(flops=40_000_000_000, bytes_accessed=12_000_000, transcendentals=0),
    )(start, x_all, stat_all, w_shard)


def bwd_kernel(steps, rows, hid, d_ref, u_ref, coef_ref, w_ref, dw_ref, db_ref, dx_ref, dx, dz_s, wrt, dbp):
    layer = pl.program_id(0)

    @pl.when(layer == 0)
    def _():
        dx[...] = d_ref[...]

    wrt[...] = w_ref[0, hid:, :].T
    dbp[...] = jnp.zeros(dbp.shape, F32)
    e_rec = jnp.zeros((rows, hid), F32)
    dc_rec = jnp.zeros((rows, hid), F32)
    for step in reversed(range(steps)):
        ts = pl.ds(step * rows, rows)
        err = dx[ts, :] + e_rec
        dct = dc_rec + err * coef_ref[0, ts, 4 * hid:5 * hid]
        e_rec = jnp.zeros((rows, hid), F32)
        for gate in range(4):
            cols = pl.ds(gate * hid, hid)
            dz = (err if gate == 3 else dct) * coef_ref[0, ts, gate * hid:(gate + 1) * hid]
            low = dz.astype(BF16)
            dz_s[ts, cols] = low
            if step:
                e_rec = e_rec + mm(low, wrt[cols, :])
            part = dz[0:8]
            for k in range(8, rows, 8):
                part = part + dz[k:k + 8]
            dbp[:, cols] += part
        dc_rec = dct * coef_ref[0, ts, 5 * hid:6 * hid]
    db_ref[0] = jnp.sum(dbp[...], axis=0, keepdims=True)
    dz_all = dz_s[...]
    dw_ref[0] = mm(u_ref[0], dz_all, ((0,), (0,)))
    dx[...] += mm(dz_all, w_ref[0, :hid, :], ((1,), (1,)))

    @pl.when(layer == pl.num_programs(0) - 1)
    def _():
        dx_ref[...] = dx[...]


def run_bwd(d_top, u_all, coef, w_lstm, steps, rows):
    layers, _, wide = w_lstm.shape
    hid = wide // 4
    tok = steps * rows
    last = layers - 1
    return pl.pallas_call(
        functools.partial(bwd_kernel, steps, rows, hid),
        grid=(layers,),
        in_specs=[
            pl.BlockSpec((tok, hid), lambda i: (0, 0)),
            pl.BlockSpec((1, tok, 2 * hid), lambda i: (last - i, 0, 0)),
            pl.BlockSpec((1, tok, 6 * hid), lambda i: (last - i, 0, 0)),
            pl.BlockSpec((1, 2 * hid, wide), lambda i: (last - i, 0, 0)),
        ],
        out_specs=[
            pl.BlockSpec((1, 2 * hid, wide), lambda i: (last - i, 0, 0)),
            pl.BlockSpec((1, 1, wide), lambda i: (last - i, 0, 0)),
            pl.BlockSpec((tok, hid), lambda i: (0, 0)),
        ],
        out_shape=[
            jax.ShapeDtypeStruct((layers, 2 * hid, wide), F32),
            jax.ShapeDtypeStruct((layers, 1, wide), F32),
            jax.ShapeDtypeStruct((tok, hid), F32),
        ],
        scratch_shapes=[
            pltpu.VMEM((tok, hid), F32),
            pltpu.VMEM((tok, wide), BF16),
            pltpu.VMEM((wide, hid), BF16),
            pltpu.VMEM((8, wide), F32),
        ],
        compiler_params=pltpu.CompilerParams(vmem_limit_bytes=VMEM_CAP),
        name='lstm_bwd',
        cost_estimate=pl.CostEstimate(flops=80_000_000_000, bytes_accessed=60_000_000, transcendentals=0),
    )(d_top, u_all, coef, w_lstm)


def solution(mesh):
    ndev = mesh.shape['data']

    def local_grads(x_rows, tgt_rows, w_lstm, b_lstm, w_vocab):
        rows, steps, hid = x_rows.shape
        tok = rows * steps
        vocab = w_vocab.shape[1]
        me = lax.axis_index('data')
        x_tok = jnp.swapaxes(x_rows, 0, 1).reshape(tok, hid)
        tgt_rep = jnp.broadcast_to(jnp.swapaxes(tgt_rows, 0, 1).reshape(tok, 1), (tok, 128))
        start = jnp.minimum(me * SHARD, vocab - SHARD)
        w_shard = lax.dynamic_slice(w_vocab, (0, start), (hid, SHARD))

        u_all, coef, x_top = run_fwd(x_tok, w_lstm, b_lstm, steps, rows)
        x_all = lax.all_gather(x_top, 'data', axis=0, tiled=True)
        d_top, stat = run_head(x_top, w_vocab, tgt_rep)
        stat_all = lax.all_gather(stat, 'data', axis=0)
        dwv = run_vocab(start.reshape(1), x_all, stat_all, w_shard)
        dwv_all = lax.all_gather(dwv, 'data', axis=0)
        tail = vocab - (ndev - 1) * SHARD
        main = jnp.swapaxes(dwv_all[:ndev - 1], 0, 1).reshape(hid, (ndev - 1) * SHARD)
        dw_vocab = jnp.concatenate([main, dwv_all[ndev - 1][:, SHARD - tail:]], axis=1)
        dw, db, dx = run_bwd(d_top, u_all, coef, w_lstm, steps, rows)
        dw, db = lax.psum((dw, db), 'data')
        dx_rows = jnp.swapaxes(dx.reshape(steps, rows, hid), 0, 1)
        return dw, db.reshape(b_lstm.shape), dw_vocab, dx_rows

    return jax.shard_map(local_grads, mesh=mesh, in_specs=(P('data'), P('data'), P(), P(), P()), out_specs=(P(), P(), P(), P('data')), check_vma=False)
```

time: 1840 us -> 668 us (0.36); the launches traced: 1810 us -> 666 us
  other arithmetic: 506 us -> 25.3 us
  waiting for transfers between devices: 673 us -> 276 us
  matrix products: 311 us -> 0 us
  Pallas kernels: 0 us -> 156 us
  local copies, waits for them, and re-layouts: 254 us -> 111 us
  blocking collectives: 43.7 us -> 84.2 us
    psum x1, waiting for transfers between devices: 673 us -> 168 us  [local_grads(): dw, db = lax.psum((dw, db), 'data')]
    dot_general x283 -> x0, matrix products: 311 us -> none  [the longest x128 141 us: time_step(): z_all = z_step + jnp.dot(h_low, w_rec, preferred_element_type=jnp.float32)]
    dynamic_update_slice x640 -> x0, other arithmetic: 226 us -> none  [the longest x512 194 us: lstm_forward(): final_state, stored = lax.scan(time_step, init_state, z_in)]
    concatenate x256 -> x1, other arithmetic: 203 us -> 25.3 us  [local_grads(): jnp.concatenate([main, dwv_all[ndev - 1][:, SHARD - tail:]], axis=1)]
    pallas_call x0 -> x4, Pallas kernels: none -> 156 us  [the longest x1 62.3 us: run_head(): pl.pallas_call(functools.partial(head_kernel, VOCAB_BLK), grid=(2, vocab...]
    squeeze x128 -> x0, local copies, waits for them, and re-layouts: 120 us -> none  [lstm_forward(): final_state, stored = lax.scan(time_step, init_state, z_in)]
    all_gather x0 -> x2, waiting for transfers between devices: none -> 108 us  [the longest x1 108 us: local_grads(): dwv_all = lax.all_gather(dwv, 'data', axis=0)]
    dynamic_update_slice x128 -> x0, local copies, waits for them, and re-layouts: 55.2 us -> none  [lstm_backward(): lax.scan(time_step, init_state, (d_out, gate_seq, c_prev_seq, tanh_seq),...]
  transfers between devices with their start and end apart: 1 -> 3, of which waited for: 1 -> 2; matrix products, arithmetic and copies ran while one was open for 0% -> 18% of each run, Pallas kernels for 0% -> 15%
where the time goes in v1:
time: 668 us; the launch traced here: 666 us
  waiting for transfers between devices  276 us (41%)
  Pallas kernels  156 us (23%)
  local copies, waits for them, and re-layouts  111 us (17%)
  blocking collectives  84.2 us (13%)
  other arithmetic  25.3 us (4%)
  between operations  13.8 us (2%)
    psum x1, waiting for transfers between devices, local_grads(): dw, db = lax.psum((dw, db), 'data')  168 us
    all_gather x1, waiting for transfers between devices, local_grads(): dwv_all = lax.all_gather(dwv, 'data', axis=0)  108 us
    pallas_call x1, Pallas kernels, run_head(): pl.pallas_call(functools.partial(head_kernel, VOCAB_BLK), grid=(2, vocab...  62.3 us
    slice x2, local copies, waits for them, and re-layouts, local_grads(): dwv_all[:ndev - 1]  55.9 us
    unnamed x5, local copies, waits for them, and re-layouts  45.7 us
    all_gather x1, blocking collectives, local_grads(): stat_all = lax.all_gather(stat, 'data', axis=0)  44.9 us
    pallas_call x1, Pallas kernels, run_bwd(): pl.pallas_call(functools.partial(bwd_kernel, steps, rows, hid), grid=(lay...  40.6 us
    psum x1, blocking collectives, local_grads(): dw, db = lax.psum((dw, db), 'data')  39.2 us
  transfers between devices with their start and end apart: 3, of which 2 were waited for; matrix products, arithmetic and copies ran while one was open for 18% of the time, Pallas kernels for 15%

profile of v1, /device:TPU:0, one launch (start us, length us, event | category | flops | bytes accessed | tf_op | source)
XLA Modules:
  0.0 665.9 jit_solution(3067304384500157719)
XLA Ops:
  7.2 0.0 all-gather.5.cloned.1.call-start
  7.2 1.4 reshape.29.b_ref
  8.6 1.7 copy.12
  10.3 0.0 copy-start
  10.3 26.9 %lstm_fwd.1 = (bf16[8,512,512]{2,1,0:T(8,128)(2,1)}, f32[8,512,1536]{2,1,0:T(8,128)}, bf16[512,256]{1,0:T(8,128)(2,1)}) custom-call(bf16[512,256]{1,0:T(8,128)(2,1)} %bitcast.22, bf16[8,512,1024]{2,1,0:T(8,128)(2,1)} %w_ref.5, f32[8,1,1024]{2,1,0:T(1,128)} %reshape.29.b_ref), custom_call_target="tpu_custom_call" | custom-call | flops 70000001024 | bytes 40000000 | tf_op jit(solution)/shard_map/lstm_fwd/pallas_call | solution.py:69
  37.2 0.0 all-gather.5.cloned.1.call-update
  37.2 0.0 all-gather.7.cloned.1.call-start
  37.3 0.0 copy-done
  37.3 0.1 broadcast_in_dim.7
  37.4 2.1 constant_dynamic-slice_fusion.w_ref
  39.5 0.9 broadcast_in_dim.8.tgt_ref
  40.3 62.3 %head.1 = (f32[512,256]{1,0:T(8,128)}, f32[8,512]{1,0:T(8,128)}) custom-call(bf16[512,256]{1,0:T(8,128)(2,1)} %get-tuple-element.12.x_ref, bf16[256,32000]{1,0:T(8,128)(2,1)} %w_ref.4, s32[512,128]{1,0:T(8,128)} %broadcast_in_dim.8.tgt_ref), custom_call_target="tpu_custom_call" | custom-call | flops 70000001024 | bytes 33000000 | tf_op jit(solution)/shard_map/head/pallas_call | solution.py:158
  102.7 44.9 %all-gather = f32[256,512]{1,0:T(8,128)} all-gather(f32[8,512]{1,0:T(8,128)} %get-tuple-element.18), channel_id=2, replica_groups=mesh['data'=32] {'data'}, dimensions={0}, use_global_device_ids=true | all-gather | bytes 540672 | tf_op jit(solution)/shard_map/all_gather | solution.py:320
  147.6 0.0 all-gather.5.cloned.1.call-done.x_ref
  147.6 25.9 %dw_vocab.1 = f32[256,1024]{1,0:T(8,128)} custom-call(s32[1]{0:T(128)} %bitcast.3.start_ref, bf16[16384,256]{1,0:T(8,128)(2,1)} %all-gather.5.cloned.1.call-done.x_ref, f32[32,8,512]{2,1,0:T(8,128)} %bitcast.20, bf16[256,1024]{1,0:T(8,128)(2,1)} %constant_dynamic-slice_fusion.w_ref), custom_call_target="tpu_custom_call" | custom-call | flops 40000000000 | bytes 12000000 | tf_op jit(solution)/shard_map/dw_vocab/pallas_call | solution.py:212
  173.5 0.0 all-gather.7.cloned.1.call-update
  173.6 0.0 all-reduce.2.cloned.1.call-start
  173.6 40.6 %lstm_bwd.1 = (f32[8,512,1024]{2,1,0:T(8,128)}, f32[8,1,1024]{2,1,0:T(1,128)}, f32[512,256]{1,0:T(8,128)}) custom-call(f32[512,256]{1,0:T(8,128)} %get-tuple-element.13.d_ref, bf16[8,512,512]{2,1,0:T(8,128)(2,1)} %get-tuple-element.14.u_ref, f32[8,512,1536]{2,1,0:T(8,128)} %get-tuple-element.15.coef_ref, bf16[8,512,1024]{2,1,0:T(8,128)(2,1)} %w_ref.5), custom_call_target="tpu_custom_call" | custom-call | flops 80000000000 | bytes 60000000 | tf_op jit(solution)/shard_map/lstm_bwd/pallas_call | solution.py:273
  214.2 0.0 all-reduce.2.cloned.1.call-update
  214.3 0.8 copy.21
  215.0 2.1 copy.20
  217.2 39.2 %psum.15 = f32[8,1024]{1,0:T(8,128)} all-reduce(f32[8,1024]{1,0:T(8,128)S(1)} %bitcast.23), channel_id=1, replica_groups=mesh['data'=32] {'data'}, use_global_device_ids=true, to_apply=%region_1.0 | all-reduce | flops 8192 | bytes 65536 | tf_op jit(solution)/shard_map/psum | solution.py:327
  256.4 107.7 %all-gather.7.cloned.1.call-done = f32[8192,1024]{1,0:T(8,128)} async-done(((f32[256,1024]{1,0:T(8,128)}), f32[8192,1024]{1,0:T(8,128)}) %all-gather.7.cloned.1.call-update) | async-done | bytes 33554448 | tf_op jit(solution)/shard_map/all_gather | solution.py:322
  364.2 23.1 %slice.15 = f32[7936,1024]{1,0:T(8,128)} slice(f32[8192,1024]{1,0:T(8,128)} %all-gather.7.cloned.1.call-done), slice={[0:7936], [0:1024]} | slice | bytes 65011712 | tf_op jit(solution)/shard_map/slice | solution.py:324
  387.3 32.8 %copy.13 = f32[31,256,1024]{1,2,0:T(8,128)} copy(f32[31,256,1024]{2,1,0:T(8,128)} %bitcast.17) | data formatting | bytes 65011712 | tf_op jit(solution)/shard_map/slice | solution.py:324
  420.0 1.0 slice.16
  421.0 0.1 copy.14
  421.1 25.3 %pad_maximum_fusion = f32[256,32000]{0,1:T(8,128)} fusion(f32[256,256]{0,1:T(8,128)S(1)} %copy.14, f32[256,31744]{0,1:T(8,128)} %bitcast.16), kind=kLoop, calls=%fused_computation | loop fusion | flops 8192000 | bytes 65536000 | tf_op jit(solution)/shard_map/concatenate | solution.py:325
  446.5 32.9 %copy.16 = f32[256,32000]{1,0:T(8,128)} copy(f32[256,32000]{0,1:T(8,128)} %pad_maximum_fusion) | data formatting | bytes 65536000
  479.4 168.0 %all-reduce.2.cloned.1.call-done = f32[8,512,1024]{2,1,0:T(8,128)} async-done(((f32[8,512,1024]{2,1,0:T(8,128)}), f32[8,512,1024]{2,1,0:T(8,128)}) %all-reduce.2.cloned.1.call-update) | async-done | bytes 16777232 | tf_op jit(solution)/shard_map/psum | solution.py:327
  647.4 12.0 %copy.23 = f32[8,512,1024]{2,1,0:T(8,128)} copy(f32[8,512,1024]{2,1,0:T(8,128)} %all-reduce.2.cloned.1.call-done) | data formatting | bytes 33554432
Async XLA Ops:
  7.2 140.4 %all-gather.5.cloned.1.call-start = ((), (), s32[]{:S(2)}) async-start(), calls=%async_computation.1 | async-start | bytes 8650752 | tf_op jit(solution)/shard_map/all_gather | solution.py:318
  10.3 26.9 %copy-start = (s32[32,16]{0,1:T(8,128)S(1)}, s32[32,16]{0,1:T(8,128)}, u32[]{:S(2)}) copy-start(s32[32,16]{0,1:T(8,128)} %param.6) | copy-start | bytes 6148
  37.2 326.9 %all-gather.7.cloned.1.call-start = ((), (), s32[]{:S(2)}) async-start(), calls=%async_computation.2 | async-start | bytes 34603008 | tf_op jit(solution)/shard_map/all_gather | solution.py:322
  173.6 473.9 %all-reduce.2.cloned.1.call-start = ((), (), s32[]{:S(2)}) async-start(), calls=%async_computation | async-start | bytes 33554432 | tf_op jit(solution)/shard_map/psum | solution.py:327
Sparse Core Ops, SparseCore 0:
  37.3 80.4 all-gather.4
  173.7 190.4 all-gather.6
  370.8 276.6 all-reduce.1

commit v2 on v1

v2 whole, which is shorter than its diff:
```python
import functools

import jax
import jax.numpy as jnp
from jax import lax
from jax.experimental import pallas as pl
from jax.experimental.pallas import tpu as pltpu
from jax.sharding import PartitionSpec as P

F32 = jnp.float32
BF16 = jnp.bfloat16
VMEM_CAP = 60 * 1024 * 1024
VOCAB_BLK = 1280
SHARD = 1024
VOCAB = 32000
LANES = 128
SUBL = 8
NSEM = 192
XPARTS = 1
XEARLY = 7


def mm(lhs, rhs, dims=((1,), (0,))):
    return lax.dot_general(lhs, rhs, (dims, ((), ())), preferred_element_type=F32)


def sig(val):
    return 0.5 * jnp.tanh(0.5 * val) + 0.5


MESH_ID = pl.DeviceIdType.MESH
SIDES = ((0, 1), (1, 0))
QUAD = ((0, 0), (0, 1), (1, 0), (1, 1))
FAR = (1, 2, 3)
HERE = (0, 0, 0, False)
LINE = (0, 1, 2, 3)


class Place:
    def __init__(self, me):
        self.me = me
        half, quarter = lax.div(me, 2), lax.div(me, 4)
        self.core, self.x, self.y, self.z = (
            lax.rem(me, 2), lax.rem(half, 2), lax.rem(quarter, 2), lax.div(me, 8))
        self.zs = [self.z, self.z + 1 - 2 * lax.rem(self.z, 2), lax.rem(self.z + 2, 4), 3 - self.z]
        self.at = {}
        for k in LINE:
            for fy, fx in QUAD:
                for other in (False, True):
                    y = 1 - self.y if fy else self.y
                    x = 1 - self.x if fx else self.x
                    c = 1 - self.core if other else self.core
                    self.at[k, fy, fx, other] = (self.zs[k], y, x, c)
        self.devs = {key: ((z * 2 + y) * 2 + x) * 2 + c for key, (z, y, x, c) in self.at.items()}
        self.partner = self.dev(0, 0, 0, True)

    def dev(self, k, fy, fx, other=False):
        return self.devs[k, fy, fx, other]

    def barrier(self):
        peers = [self.dev(k, 0, 0) for k in FAR] + [self.dev(0, *side) for side in SIDES] + [self.partner]
        sem = pltpu.get_barrier_semaphore()
        for peer in peers:
            pl.semaphore_signal(sem, device_id=(peer,), device_id_type=MESH_ID)
        pl.semaphore_wait(sem, len(peers))


class Link:
    def __init__(self, send, recv):
        self.send, self.recv, self.keys = send, recv, {}

    def copy(self, key, src, dst, peer):
        at = self.keys.setdefault(key, len(self.keys))
        return pltpu.make_async_remote_copy(
            src_ref=src, dst_ref=dst, send_sem=self.send.at[at], recv_sem=self.recv.at[at],
            device_id=(peer,), device_id_type=MESH_ID)


class Gather:
    def __init__(self, place, link, name, own, slot, half):
        self.p, self.link, self.name, self.own, self.slot, self.half = place, link, name, own, slot, half
        self.sent = []

    def _send(self, key, at, to, other=False, half=None):
        at = at + (False,)

        def make():
            if half is None:
                dst = self.slot(at)
                src = dst if any(at) else self.own
            else:
                src = dst = self.half(at, half)
            return self.link.copy((self.name,) + key, src, dst, self.p.dev(*to, other))

        self.sent.append(make)
        make().start()

    def _arrive(self, key, at, other=False, half=None):
        at = at + (other,)
        ref = self.slot(at) if half is None else self.half(at, half)
        self.link.copy((self.name,) + key, ref, ref, self.p.partner).wait_recv()

    def _pair(self, *at):
        self._send(('pair',) + at, at, LINE[:1] + QUAD[0], True)

    def _line(self, k):
        for side in SIDES:
            self._send(('line', k) + side, (k, 0, 0), (0,) + side)

    def _far(self):
        for k in FAR:
            self._send(('far', k), LINE[:1] + QUAD[0], (k,) + QUAD[0])

    def start(self):
        self._line(0)
        self._far()
        self._pair(0, 0, 0)

    def take_far(self, k):
        self._arrive(('far', k), (k,) + QUAD[0])
        self._line(k)
        self._pair(k, *QUAD[0])

    def take_line(self, k):
        for h, side in enumerate(SIDES):
            self._arrive(('line', k) + side, (k,) + side)
            self._send(('diag', k, h), (k,) + side, (0,) + SIDES[1 - h], half=h)
            self._pair(k, *side)

    def take_diag(self, k):
        for h in range(2):
            self._arrive(('diag', k, h), (k,) + QUAD[3], half=h)
        self._pair(k, *QUAD[3])

    def finish(self):
        for k in LINE:
            for side in QUAD:
                self._arrive(('pair', k) + side, (k,) + side, True)
        for make in self.sent:
            make().wait_send()

    def steps(self):
        far = [functools.partial(self.take_far, k) for k in LINE]
        line = [functools.partial(self.take_line, k) for k in LINE]
        diag = [functools.partial(self.take_diag, k) for k in LINE]
        return [far[1], line[0], far[2], line[1], far[3], diag[0], line[2], diag[1], line[3]] + diag[2:]


def fwd_kernel(steps, rows, hid, x_ref, w_ref, b_ref, u_ref, coef_ref, top_ref, xs, zin):
    layer = pl.program_id(0)

    @pl.when(layer == 0)
    def _():
        xs[...] = x_ref[...]

    x_val = xs[...]
    u_ref[0, :, :hid] = x_val
    zin[...] = mm(x_val, w_ref[0, :hid, :]) + b_ref[pl.ds(layer, 1), :]
    h_low = jnp.zeros((rows, hid), BF16)
    cell = jnp.zeros((rows, hid), F32)
    for step in range(steps):
        ts = pl.ds(step * rows, rows)
        u_ref[0, ts, hid:] = h_low
        z_all = zin[ts, :]
        if step:
            z_all = z_all + mm(h_low, w_ref[0, hid:, :])
        gi = sig(z_all[:, :hid])
        gf = sig(z_all[:, hid:2 * hid])
        gg = jnp.tanh(z_all[:, 2 * hid:3 * hid])
        go = sig(z_all[:, 3 * hid:])
        c_new = gf * cell + gi * gg
        tc = jnp.tanh(c_new)
        h_new = go * tc
        h_low = h_new.astype(BF16)
        coefs = (gg * gi * (1.0 - gi), cell * gf * (1.0 - gf), gi * (1.0 - gg * gg), tc * go * (1.0 - go),
                 go * (1.0 - tc * tc), gf)
        for at, val in enumerate(coefs):
            coef_ref[0, ts, at * hid:(at + 1) * hid] = val
        cell = c_new
        xs[ts, :] = (xs[ts, :].astype(F32) + h_new).astype(BF16)

    @pl.when(layer == pl.num_programs(0) - 1)
    def _():
        top_ref[...] = xs[...]


def run_fwd(x_tok, w_lstm, b_lstm, steps, rows):
    layers, _, wide = w_lstm.shape
    hid = wide // 4
    tok = steps * rows
    return pl.pallas_call(
        functools.partial(fwd_kernel, steps, rows, hid),
        grid=(layers,),
        in_specs=[
            pl.BlockSpec((tok, hid), lambda i: (0, 0)),
            pl.BlockSpec((1, 2 * hid, wide), lambda i: (i, 0, 0)),
            pl.BlockSpec((layers, wide), lambda i: (0, 0)),
        ],
        out_specs=[
            pl.BlockSpec((1, tok, 2 * hid), lambda i: (i, 0, 0)),
            pl.BlockSpec((1, tok, 6 * hid), lambda i: (i, 0, 0)),
            pl.BlockSpec((tok, hid), lambda i: (0, 0)),
        ],
        out_shape=[
            jax.ShapeDtypeStruct((layers, tok, 2 * hid), BF16),
            jax.ShapeDtypeStruct((layers, tok, 6 * hid), F32),
            jax.ShapeDtypeStruct((tok, hid), BF16),
        ],
        scratch_shapes=[pltpu.VMEM((tok, hid), BF16), pltpu.VMEM((tok, wide), F32)],
        compiler_params=pltpu.CompilerParams(vmem_limit_bytes=VMEM_CAP),
        name='lstm_fwd',
        cost_estimate=pl.CostEstimate(flops=70_000_000_000, bytes_accessed=40_000_000, transcendentals=0),
    )(x_tok, w_lstm, b_lstm)


def head_kernel(blk, x_ref, w_ref, tgt_ref, xall_ref, sall_ref, m_ref, r_ref, m_s, s_s, stat_s, ssem, rsem, lsem):
    blk_id = pl.program_id(0)
    last = pl.num_programs(0) - 1
    tok = x_ref.shape[0]
    place = Place(lax.axis_index('data'))
    link = Link(ssem, rsem)
    mid = tok // 2

    def chunk_at(part):
        num = tok // XPARTS
        row = lambda dev, h, n: pl.ds(pl.multiple_of(dev * tok + part * num + h * n, n), n)
        return Gather(place, link, ('x', part), x_ref.at[pl.ds(part * num, num), :],
                      lambda at: xall_ref.at[row(place.devs[at], 0, num), :],
                      lambda at, h: xall_ref.at[row(place.devs[at], h, num // 2), :])

    gats = [chunk_at(part) for part in range(XPARTS)]
    gat_s = Gather(place, link, 's', stat_s, lambda at: sall_ref.at[place.devs[at]],
                   lambda at, h: sall_ref.at[place.devs[at], :, pl.ds(h * mid, mid)])
    loc_x = [pltpu.make_async_copy(g.own, g.slot(HERE), lsem.at[1 + at]) for at, g in enumerate(gats)]
    loc_s = pltpu.make_async_copy(stat_s, gat_s.slot(HERE), lsem.at[0])
    sx, ss = [act for acts in zip(*[g.steps() for g in gats]) for act in acts], gat_s.steps()

    @pl.when(blk_id == 0)
    def _():
        place.barrier()
        for gat, loc in zip(gats, loc_x):
            gat.start()
            loc.start()
        m_s[...] = jnp.full(m_s.shape, -jnp.inf, F32)
        s_s[...] = jnp.zeros(s_s.shape, F32)

    for at, act in zip(range(6, VOCAB // blk - 1), sx[:XEARLY]):
        pl.when(blk_id == at)(act)

    for r0 in range(0, tok, LANES):
        rs = pl.ds(r0, LANES)
        logits = mm(x_ref[rs, :], w_ref[...])
        cols = [logits[:, k:k + LANES] for k in range(0, blk, LANES)]
        m_old = m_s[rs, :]
        m_new = functools.reduce(jnp.maximum, cols, m_old)
        tot = s_s[rs, :] * jnp.exp(m_old - m_new)
        for col in cols:
            tot = tot + jnp.exp(col - m_new)
        m_s[rs, :] = m_new
        s_s[rs, :] = tot

    @pl.when(blk_id == last)
    def _():
        m_lane = m_s[...]
        m_row = jnp.max(m_lane, axis=1, keepdims=True)
        s_row = jnp.sum(s_s[...] * jnp.exp(m_lane - m_row), axis=1, keepdims=True)
        m_rep = jnp.broadcast_to(m_row, m_lane.shape)
        r_rep = jnp.broadcast_to(1.0 / s_row, m_lane.shape)
        m_ref[...] = m_rep
        r_ref[...] = r_rep
        stat_s[...] = jnp.zeros(stat_s.shape, F32)
        for at, val in enumerate((m_rep, r_rep, tgt_ref[...].astype(F32))):
            stat_s[at:at + 1, :] = val.T[:1, :]
        gat_s.start()
        loc_s.start()
        for at in range(len(ss)):
            for act in sx[XEARLY + at:XEARLY + at + 1] + ss[at:at + 1]:
                act()
        for act in sx[XEARLY + len(ss):]:
            act()
        for gat in gats + [gat_s]:
            gat.finish()
        for loc in loc_x + [loc_s]:
            loc.wait()


def run_head(x_top, w_vocab, tgt_rep, ndev):
    tok, hid = x_top.shape
    full = pl.BlockSpec(memory_space=pltpu.VMEM)
    anyw = pl.BlockSpec(memory_space=pl.ANY)
    stat = jax.ShapeDtypeStruct((tok, LANES), F32)
    same = pl.BlockSpec((tok, LANES), lambda j: (0, 0))
    return pl.pallas_call(
        functools.partial(head_kernel, VOCAB_BLK),
        grid=(VOCAB // VOCAB_BLK,),
        in_specs=[full, pl.BlockSpec((hid, VOCAB_BLK), lambda j: (0, j)), full],
        out_specs=[anyw, anyw, same, same],
        out_shape=[
            jax.ShapeDtypeStruct((ndev * tok, hid), BF16),
            jax.ShapeDtypeStruct((ndev, SUBL, tok), F32), stat, stat,
        ],
        scratch_shapes=[
            pltpu.VMEM((tok, LANES), F32), pltpu.VMEM((tok, LANES), F32), pltpu.VMEM((SUBL, tok), F32),
            pltpu.SemaphoreType.DMA((LANES,)), pltpu.SemaphoreType.DMA((LANES,)), pltpu.SemaphoreType.DMA((1 + XPARTS,)),
        ],
        compiler_params=pltpu.CompilerParams(vmem_limit_bytes=VMEM_CAP, collective_id=1, has_side_effects=True),
        name='head',
        cost_estimate=pl.CostEstimate(flops=10**10, bytes_accessed=10**7, transcendentals=0),
    )(x_top, w_vocab, tgt_rep)


GROUP = 4
SPLIT = 2
WID = SHARD // SPLIT
TOK_BLK = 1024


class Reduce:
    def __init__(self, place, link, grp, buf, boxes):
        self.p, self.link, self.grp, self.buf, self.boxes = place, link, grp, buf, boxes
        self.first = grp * GROUP
        self.lay = pl.ds(self.first, GROUP)
        p = place
        xdev, ydev = p.dev(0, *SIDES[0]), p.dev(0, *SIDES[1])
        pick = lambda one, two: (1 - p.core) * one + p.core * two
        self.peers = [p.partner, pick(xdev, ydev), pick(ydev, xdev)]
        self.give, self.keep, self.size, base = [], [], [], 0
        for at, bit in enumerate((p.core, pick(p.x, p.y), pick(p.y, p.x))):
            size = buf.shape[1] >> (at + 1)
            self.size.append(size)
            self.give.append(base + (1 - bit) * size)
            base = base + bit * size
            self.keep.append(base)
        self.unit = size // len(LINE)
        self.base = base
        self.sent = []

    def _rows(self, start, num):
        return pl.ds(pl.multiple_of(start, num), num)

    def _copies(self, at):
        if at < len(self.size):
            src = self.buf.at[self.lay, self._rows(self.give[at], self.size[at]), :]
            return [self.link.copy(('sum', self.grp, at), src, self.boxes[at].at[self.lay], self.peers[at])]
        out = []
        for k in FAR:
            src = self.buf.at[self.lay, self._rows(self.base + self.p.zs[k] * self.unit, self.unit), :]
            dst = self.boxes[at].at[k - 1, self.lay]
            out.append(self.link.copy(('sum', self.grp, at, k), src, dst, self.p.dev(k, 0, 0)))
        return out

    def start(self, at=0):
        for copy in self._copies(at):
            copy.start()

    def take(self, at):
        for copy in self._copies(at):
            copy.wait_recv()
        far = at == len(self.size)
        num = self.unit if far else self.size[at]
        rows = self._rows(self.base + self.p.z * num if far else self.keep[at], num)
        for i in range(GROUP):
            lay = self.first + i
            val = self.buf[lay, rows, :]
            for k in FAR if far else FAR[:1]:
                val = val + (self.boxes[at][k - 1, lay] if far else self.boxes[at][lay])
            self.buf[lay, rows, :] = val
        if not far:
            self.start(at + 1)

    def finish(self):
        for at in LINE:
            for copy in self._copies(at):
                copy.wait_send()


def main_kernel(phases, steps, rows, hid, x_ref, stat_ref, wv_ref, wsh_ref, m_ref, r_ref, tgt_ref, xl_ref,
                u_ref, coef_ref, w_ref, dw_ref, db_ref, dx_ref, dv_ref,
                wt, acc, shv, dx, dz_s, wrt, dbp, buf, r0, r1, r2, r3, dbb, dball, gs, gr, ls):
    step_id = pl.program_id(0)
    n_vocab, n_top, n_layers = phases
    t_top = n_vocab
    t_bwd = n_vocab + n_top
    t_last = t_bwd + n_layers - 1
    place = Place(lax.axis_index('data'))
    link = Link(gs, gr)
    ndev = stat_ref.shape[0] * n_vocab // SPLIT
    tail = dball.shape[0] - 1

    def chunk_at(q):
        cols = lambda at: pl.ds(pl.multiple_of(place.devs[at] * SHARD + q * WID, WID), WID)
        return Gather(
            place, link, ('v', q), shv.at[q], lambda at: dv_ref.at[:, cols(at)],
            lambda at, h: dv_ref.at[pl.ds(h * (hid // 2), hid // 2), cols(at)])

    def piece(at):
        z, y, x, c = place.at[at]
        far, near = hid // 2, hid // 4
        return c * hid + ((1 - c) * x + c * y) * far + ((1 - c) * y + c * x) * near + z * (near // 4)

    pieces = {at: piece(at) for at in place.at}

    def group_at(grp):
        lay = pl.ds(grp * GROUP, GROUP)
        unit = hid // 16
        part = lambda at, h, n: pl.ds(pl.multiple_of(pieces[at] + h * n, n), n)
        return Gather(
            place, link, ('w', grp), buf.at[lay, part(HERE, 0, unit), :],
            lambda at: dw_ref.at[lay, part(at, 0, unit), :],
            lambda at, h: dw_ref.at[lay, part(at, h, unit // 2), :])

    gats = [chunk_at(q) for q in range(SPLIT)]
    n_grp = n_layers // GROUP
    reds = [Reduce(place, link, n_grp - 1 - j, buf, (r0, r1, r2, r3)) for j in range(n_grp)]
    outs = [group_at(n_grp - 1 - j) for j in range(n_grp)]
    wide2 = dbb.shape[1] // 2
    gdb = Gather(place, link, 'b', dbb, lambda at: dball.at[place.devs[at]],
                 lambda at, h: dball.at[place.devs[at], :, pl.ds(h * wide2, wide2)])
    own_v = [pltpu.make_async_copy(shv.at[q], gats[q].slot(HERE), ls.at[q]) for q in range(SPLIT)]
    own_w = [pltpu.make_async_copy(outs[g].own, outs[g].slot(HERE), ls.at[SPLIT + g]) for g in range(n_grp)]
    def slot_of(when):
        if when >= t_top:
            when = t_top + (when - t_top) * 5 // SUBL
        return when if when < t_bwd else t_bwd + (when - t_bwd) // 4

    per_chunk = n_vocab // SPLIT
    todo = sorted(
        (per_chunk * (q + 1) + 6 + 9 * n, q, n) for q in range(SPLIT) for n in range(len(gats[q].steps())))
    acts = [(slot_of(when), gats[q].steps()[n]) for when, q, n in todo]

    def emit(j):
        reds[j].take(3)
        outs[j].start()
        own_w[j].start()

    late = []
    for j in range(n_grp):
        ops = [functools.partial(reds[j].take, n) for n in range(3)] + [functools.partial(emit, j)]
        late += [(n, j, op) for n, op in enumerate(ops)]
        late += [(4 + n, j, op) for n, op in enumerate(outs[j].steps())]
    late += [(4 * n_grp + n, n_grp, op) for n, op in enumerate(gdb.steps())]
    late = [op for _, _, op in sorted(late, key=lambda item: item[:2])]

    @pl.when(step_id == 0)
    def _():
        place.barrier()
        wt[...] = wsh_ref[...].T
        dx[...] = jnp.zeros(dx.shape, F32)

    per = n_vocab // SPLIT
    q_now, blk_now = lax.div(step_id, per), lax.rem(step_id, per)

    @pl.when((step_id < t_top) & (blk_now == 0))
    def _():
        acc[...] = jnp.zeros(acc.shape, F32)

    @pl.when(step_id < t_top)
    def _():
        m_row, r_row, tgt = [
            jnp.concatenate([stat_ref[p, r:r + 1, :] for p in range(stat_ref.shape[0])], axis=1) for r in range(3)]
        x_val = x_ref[...]
        logits = mm(wt[pl.ds(pl.multiple_of(q_now * WID, WID), WID), :], x_val, ((1,), (1,)))
        prob = jnp.exp(logits - m_row) * r_row
        ids = lax.broadcasted_iota(jnp.int32, prob.shape, 0) + (place.me * SHARD + q_now * WID)
        dist = ids.astype(F32) - tgt
        hot = jnp.maximum(1.0 - jnp.maximum(dist, -dist), 0.0)
        acc[...] += mm((prob - hot).astype(BF16), x_val)

    for k in range(SPLIT):
        @pl.when(step_id == k * per + per - 1)
        def _(k=k):
            shv[k] = acc[...].T
            gats[k].start()
            own_v[k].start()

    for at, act in acts:
        if at < t_last:
            pl.when(step_id == at)(act)

    @pl.when((step_id >= t_top) & (step_id < t_bwd))
    def _():
        blk = wv_ref.shape[1]
        lane_id = lax.broadcasted_iota(jnp.int32, (LANES, LANES), 1) + (step_id - t_top) * blk

        @pl.loop(0, dx.shape[0] // LANES)
        def _(part):
            rs = pl.ds(pl.multiple_of(part * LANES, LANES), LANES)
            logits = mm(xl_ref[rs, :], wv_ref[...])
            m_row, r_row = m_ref[rs, :], r_ref[rs, :]
            off = tgt_ref[rs, :] - lane_id
            pieces = []
            for k in range(0, blk, LANES):
                prob = jnp.exp(logits[:, k:k + LANES] - m_row) * r_row
                pieces.append(jnp.where(off == k, prob - 1.0, prob).astype(BF16))
            dx[rs, :] += mm(jnp.concatenate(pieces, axis=1), wv_ref[...], ((1,), (1,)))

    @pl.when(step_id >= t_bwd)
    def _():
        lay = t_last - step_id
        wrt[...] = w_ref[0, hid:, :].T
        dbp[...] = jnp.zeros(dbp.shape, F32)
        e_rec = jnp.zeros((rows, hid), F32)
        dc_rec = jnp.zeros((rows, hid), F32)
        for step in reversed(range(steps)):
            ts = pl.ds(step * rows, rows)
            coef = [coef_ref[0, ts, at * hid:(at + 1) * hid] for at in range(6)]
            err = dx[ts, :] + e_rec
            dct = dc_rec + err * coef[4]
            e_rec = jnp.zeros((rows, hid), F32)
            for gate in LINE:
                cols = pl.ds(gate * hid, hid)
                dz = (err if gate == LINE[-1] else dct) * coef[gate]
                low = dz.astype(BF16)
                dz_s[ts, cols] = low
                if step:
                    e_rec = e_rec + mm(low, wrt[cols, :])
                dbp[:, cols] += functools.reduce(jnp.add, [dz[k:k + SUBL] for k in range(0, rows, SUBL)])
            dc_rec = dct * coef[5]
        dbb[pl.ds(lay, 1), :] = jnp.sum(dbp[...], axis=0, keepdims=True)
        dz_all = dz_s[...]
        buf[lay] = mm(u_ref[0], dz_all, ((0,), (0,)))
        dx[...] += mm(dz_all, w_ref[0, :hid, :], ((1,), (1,)))

    for j in range(n_grp):
        pl.when(step_id == t_bwd + GROUP * (j + 1) - 1)(reds[j].start)

    done = 0
    for at, upto in ((4, 1),):
        for act in late[done:upto]:
            pl.when(step_id == t_bwd + at)(act)
        done = upto

    @pl.when(step_id == t_last)
    def _():
        dx_ref[...] = dx[...]
        gdb.start()
        rest = [act for at, act in acts if at >= t_last]
        for at in range(len(late) - done):
            for act in rest[at:at + 1] + late[done + at:done + at + 1]:
                act()
        for act in rest[len(late) - done:]:
            act()
        dball[place.me] = dbb[...]
        gdb.finish()
        total = dball[0]
        for dev in range(1, tail + 1):
            total = total + dball[dev]
        db_ref[...] = total
        for gat in gats + outs:
            gat.finish()
        for q in range(SPLIT):
            own_v[q].wait()
        for copy in own_w:
            copy.wait()
        for red in reds:
            red.finish()


def run_main(x_all, stat_all, w_vocab, w_shard, m_rep, r_rep, tgt_rep, x_last, u_all, coef, w_lstm, steps, rows, ndev):
    layers, _, wide = w_lstm.shape
    hid = wide // 4
    tok = steps * rows
    blocks = ndev * tok // TOK_BLK
    phases = (SPLIT * blocks, VOCAB // VOCAB_BLK, layers)
    t_top = phases[0]
    t_bwd = t_top + phases[1]
    full = pl.BlockSpec(memory_space=pltpu.VMEM)
    anyw = pl.BlockSpec(memory_space=pl.ANY)
    total = sum(phases)
    past = lambda i, at: (i + total - at) // total
    at_tok = lambda i: (1 - past(i, t_top)) * (i % blocks) + past(i, t_top) * (blocks - 1)
    at_voc = lambda i: past(i, t_top) * (1 - past(i, t_bwd)) * (i - t_top) + past(i, t_bwd) * (phases[1] - 1)
    at_lay = lambda i: layers - 1 - past(i, t_bwd) * (i - t_bwd)
    same = lambda shape: pl.BlockSpec(shape, lambda i: (0, 0))
    sem = pltpu.SemaphoreType.DMA
    return pl.pallas_call(
        functools.partial(main_kernel, phases, steps, rows, hid),
        grid=(total,),
        in_specs=[
            pl.BlockSpec((TOK_BLK, hid), lambda i: (at_tok(i), 0)),
            pl.BlockSpec((TOK_BLK // tok, SUBL, tok), lambda i: (at_tok(i), 0, 0)),
            pl.BlockSpec((hid, VOCAB_BLK), lambda i: (0, at_voc(i))),
            full, full, full, full, full,
            pl.BlockSpec((1, tok, 2 * hid), lambda i: (at_lay(i), 0, 0)),
            pl.BlockSpec((1, tok, 6 * hid), lambda i: (at_lay(i), 0, 0)),
            pl.BlockSpec((1, 2 * hid, wide), lambda i: (at_lay(i), 0, 0)),
        ],
        out_specs=[anyw, same((layers, wide)), same((tok, hid)), anyw],
        out_shape=[
            jax.ShapeDtypeStruct((layers, 2 * hid, wide), F32),
            jax.ShapeDtypeStruct((layers, wide), F32),
            jax.ShapeDtypeStruct((tok, hid), F32),
            jax.ShapeDtypeStruct((hid, ndev * SHARD), F32),
        ],
        scratch_shapes=[
            pltpu.VMEM((SHARD, hid), BF16),
            pltpu.VMEM((WID, hid), F32),
            pltpu.VMEM((SPLIT, hid, WID), F32),
            pltpu.VMEM((tok, hid), F32),
            pltpu.VMEM((tok, wide), BF16),
            pltpu.VMEM((wide, hid), BF16),
            pltpu.VMEM((SUBL, wide), F32),
            pltpu.VMEM((layers, 2 * hid, wide), F32),
            pltpu.VMEM((layers, hid, wide), F32),
            pltpu.VMEM((layers, hid // 2, wide), F32),
            pltpu.VMEM((layers, hid // 4, wide), F32),
            pltpu.VMEM((3, layers, hid // 16, wide), F32),
            pltpu.VMEM((layers, wide), F32),
            pltpu.VMEM((ndev, layers, wide), F32),
            sem((NSEM,)), sem((NSEM,)), sem((SPLIT + layers // GROUP,)),
        ],
        compiler_params=pltpu.CompilerParams(vmem_limit_bytes=VMEM_CAP, collective_id=2, has_side_effects=True),
        name='main',
        cost_estimate=pl.CostEstimate(flops=10**10, bytes_accessed=10**7, transcendentals=0),
    )(x_all, stat_all, w_vocab, w_shard, m_rep, r_rep, tgt_rep, x_last, u_all, coef, w_lstm)


def solution(mesh):
    ndev = mesh.shape['data']

    def local_grads(x_rows, tgt_rows, w_lstm, b_lstm, w_vocab):
        rows, steps, hid = x_rows.shape
        tok = rows * steps
        x_tok = jnp.swapaxes(x_rows, 0, 1).reshape(tok, hid)
        tgt_rep = jnp.broadcast_to(jnp.swapaxes(tgt_rows, 0, 1).reshape(tok, 1), (tok, LANES))
        me = lax.axis_index('data')
        start = jnp.minimum(me * SHARD, VOCAB - SHARD)
        w_shard = lax.dynamic_slice(w_vocab, (0, start), (hid, SHARD))
        w_shard = jnp.where(me == ndev - 1, jnp.roll(w_shard, VOCAB - ndev * SHARD, axis=1), w_shard)
        u_all, coef, x_last = run_fwd(x_tok, w_lstm, b_lstm, steps, rows)
        x_all, stat_all, m_rep, r_rep = run_head(x_last, w_vocab, tgt_rep, ndev)
        dw, db, dx, dv = run_main(x_all, stat_all, w_vocab, w_shard, m_rep, r_rep, tgt_rep, x_last, u_all, coef, w_lstm, steps, rows, ndev)
        dx_rows = jnp.swapaxes(dx.reshape(steps, rows, hid), 0, 1)
        return dw, db, dv[:, :VOCAB], dx_rows

    return jax.shard_map(local_grads, mesh=mesh, in_specs=(P('data'), P('data'), P(), P(), P()), out_specs=(P(), P(), P(), P('data')), check_vma=False)
```

time: 668 us -> 499 us (0.75)
  Pallas kernels: 156 us -> 456 us
  waiting for transfers between devices: 276 us -> 0 us
  blocking collectives: 84.2 us -> 0 us
  local copies, waits for them, and re-layouts: 111 us -> 39.7 us
  other arithmetic: 25.3 us -> 2.16 us
  between operations: 13.8 us -> 0.71 us
    pallas_call x3 -> x2, Pallas kernels: 129 us -> 429 us  [the longest x1 367 us: run_main(): pl.pallas_call(functools.partial(main_kernel, phases, steps, rows, hid),...]
    psum x1 -> x0, waiting for transfers between devices: 168 us -> none  [local_grads(): dw, db = lax.psum((dw, db), 'data')]
    all_gather x2 -> x0, waiting for transfers between devices: 108 us -> none  [the longest x1 108 us: local_grads(): dwv_all = lax.all_gather(dwv, 'data', axis=0)]
    all_gather x1 -> x0, blocking collectives: 44.9 us -> none  [local_grads(): stat_all = lax.all_gather(stat, 'data', axis=0)]
    psum x1 -> x0, blocking collectives: 39.2 us -> none  [local_grads(): dw, db = lax.psum((dw, db), 'data')]
    unnamed x5 -> x12, local copies, waits for them, and re-layouts: 45.7 us -> 6.8 us
    slice x4 -> x3, local copies, waits for them, and re-layouts: 57 us -> 27.2 us  [the longest x1 25 us: local_grads(): return (dw, db, dv[:, :VOCAB], dx_rows)]
    concatenate x1 -> x0, other arithmetic: 25.3 us -> none  [local_grads(): jnp.concatenate([main, dwv_all[ndev - 1][:, SHARD - tail:]], axis=1)]
  transfers between devices with their start and end apart: 3 -> 0, of which waited for: 2 -> 0; matrix products, arithmetic and copies ran while one was open for 18% -> 0% of each run, Pallas kernels for 15% -> 0%
where the time goes in v2:
time: 499 us; the launch traced here: 498 us
  Pallas kernels  456 us (91%)
  local copies, waits for them, and re-layouts  39.7 us (8%)
    pallas_call x1, Pallas kernels, run_main(): pl.pallas_call(functools.partial(main_kernel, phases, steps, rows, hid),...  367 us
    pallas_call x1, Pallas kernels, run_head(): pl.pallas_call(functools.partial(head_kernel, VOCAB_BLK), grid=(VOCAB //...  62.2 us
    pallas_call x1, Pallas kernels, run_fwd(): pl.pallas_call(functools.partial(fwd_kernel, steps, rows, hid), grid=(lay...  26.8 us
    slice x1, local copies, waits for them, and re-layouts, local_grads(): return (dw, db, dv[:, :VOCAB], dx_rows)  25 us

profile of v2, /device:TPU:0, one launch (start us, length us, event | category | flops | bytes accessed | tf_op | source)
XLA Modules:
  0.0 498.3 jit_solution(13589449075885388300)
XLA Ops:
  0.6 0.8 broadcast_in_dim.7
  1.4 1.0 constant_dynamic-slice_fusion.1
  2.5 0.8 broadcast_in_dim.8.tgt_ref
  3.3 1.7 copy.9
  5.0 1.2 constant_dynamic-slice_fusion
  6.2 2.2 maximum_select_fusion.wsh_ref
  8.4 26.8 %lstm_fwd.1 = (bf16[8,512,512]{2,1,0:T(8,128)(2,1)}, f32[8,512,1536]{2,1,0:T(8,128)}, bf16[512,256]{1,0:T(8,128)(2,1)}) custom-call(bf16[512,256]{1,0:T(8,128)(2,1)} %bitcast.12, bf16[8,512,1024]{2,1,0:T(8,128)(2,1)} %w_ref.5, f32[8,1024]{1,0:T(8,128)} %b_ref.1), custom_call_target="tpu_custom_call" | custom-call | flops 70000001024 | bytes 40000000 | tf_op jit(solution)/shard_map/lstm_fwd/pallas_call | solution.py:191
  35.2 62.2 %head.1 = (bf16[16384,256]{1,0:T(8,128)(2,1)}, f32[32,8,512]{2,1,0:T(8,128)}, f32[512,128]{1,0:T(8,128)}, f32[512,128]{1,0:T(8,128)}) custom-call(bf16[512,256]{1,0:T(8,128)(2,1)} %get-tuple-element.15.x_ref.xl_ref, bf16[256,32000]{1,0:T(8,128)(2,1)} %wv_ref.1, s32[512,128]{1,0:T(8,128)} %broadcast_in_dim.8.tgt_ref), custom_call_target="tpu_custom_call" | custom-call | flops 10000000000 | bytes 10000000 | tf_op jit(solution)/shard_map/head/pallas_call | solution.py:293
  97.4 366.7 %main.1 = (f32[8,512,1024]{2,1,0:T(8,128)}, f32[8,1024]{1,0:T(8,128)}, f32[512,256]{1,0:T(8,128)}, f32[256,32768]{1,0:T(8,128)}) custom-call(bf16[16384,256]{1,0:T(8,128)(2,1)} %get-tuple-element.16.x_ref, f32[32,8,512]{2,1,0:T(8,128)} %get-tuple-element.17.stat_ref, bf16[256,32000]{1,0:T(8,128)(2,1)} %wv_ref.1, ...), custom_call_target="tpu_custom_call" | custom-call | flops 10000000000 | bytes 10000000 | tf_op jit(solution)/shard_map/main/pallas_call | solution.py:576
  464.1 0.0 slice-start
  464.1 2.3 copy.12
  466.4 0.0 slice-start.1
  466.4 0.0 slice-start.2
  466.4 0.0 slice-start.3
  466.4 25.0 %slice.13 = f32[256,32000]{1,0:T(8,128)} slice(f32[256,32768]{1,0:T(8,128)} %get-tuple-element.24), slice={[0:256], [0:32000]} | slice | bytes 65536000 | tf_op jit(solution)/shard_map/slice | solution.py:634
  491.4 0.0 slice-done
  491.4 0.0 slice-done.1
  491.4 0.0 slice-done.2
  491.4 0.0 slice-done.3
  491.5 0.0 copy-start
  491.5 6.2 %copy.15 = f32[8,512,1024]{2,1,0:T(8,128)} copy(f32[8,512,1024]{2,1,0:T(8,128)S(1)} %bitcast.8) | data formatting | bytes 33554432
  497.6 0.0 copy-done
  497.6 0.6 copy.16
  (1 shorter events, 0.0 us)
Async XLA Ops:
  464.1 27.3 %slice-start = ((s8[16777216]{0:T(1024)(128)(4,1)}), s8[4194304]{0:T(1024)(128)(4,1)S(1)}, s32[]{:S(2)}) async-start(s8[16777216]{0:T(1024)(128)(4,1)} %bitcast.7), calls=%async_computation | async-start | bytes 8388608
  466.4 25.0 %slice-start.1 = ((s8[16777216]{0:T(1024)(128)(4,1)}), s8[4194304]{0:T(1024)(128)(4,1)S(1)}, s32[]{:S(2)}) async-start(s8[16777216]{0:T(1024)(128)(4,1)} %bitcast.7), calls=%async_computation.1 | async-start | bytes 8388608
  466.4 25.0 %slice-start.2 = ((s8[16777216]{0:T(1024)(128)(4,1)}), s8[4194304]{0:T(1024)(128)(4,1)S(1)}, s32[]{:S(2)}) async-start(s8[16777216]{0:T(1024)(128)(4,1)} %bitcast.7), calls=%async_computation.2 | async-start | bytes 8388608
  466.4 25.0 %slice-start.3 = ((s8[16777216]{0:T(1024)(128)(4,1)}), s8[4194304]{0:T(1024)(128)(4,1)S(1)}, s32[]{:S(2)}) async-start(s8[16777216]{0:T(1024)(128)(4,1)} %bitcast.7), calls=%async_computation.3 | async-start | bytes 8388608
  491.5 6.2 %copy-start = (f32[8,1024]{1,0:T(8,128)S(1)}, f32[8,1024]{1,0:T(8,128)}, u32[]{:S(2)}) copy-start(f32[8,1024]{1,0:T(8,128)} %get-tuple-element.31) | copy-start | bytes 98308

commit v3 on v2

--- a/solution.py
+++ b/solution.py
@@ -15,9 +15,9 @@
 VOCAB = 32000
 LANES = 128
 SUBL = 8
-NSEM = 192
-XPARTS = 1
-XEARLY = 7
+NSEM = 384
+XPARTS = 2
+XEARLY = 14
 
 
 def mm(lhs, rhs, dims=((1,), (0,))):
@@ -247,17 +247,15 @@
     for at, act in zip(range(6, VOCAB // blk - 1), sx[:XEARLY]):
         pl.when(blk_id == at)(act)
 
-    for r0 in range(0, tok, LANES):
-        rs = pl.ds(r0, LANES)
-        logits = mm(x_ref[rs, :], w_ref[...])
-        cols = [logits[:, k:k + LANES] for k in range(0, blk, LANES)]
-        m_old = m_s[rs, :]
-        m_new = functools.reduce(jnp.maximum, cols, m_old)
-        tot = s_s[rs, :] * jnp.exp(m_old - m_new)
-        for col in cols:
-            tot = tot + jnp.exp(col - m_new)
-        m_s[rs, :] = m_new
-        s_s[rs, :] = tot
+    logits = mm(x_ref[...], w_ref[...])
+    cols = [logits[:, k:k + LANES] for k in range(0, blk, LANES)]
+    m_old = m_s[...]
+    m_new = functools.reduce(jnp.maximum, cols, m_old)
+    tot = s_s[...] * jnp.exp(m_old - m_new)
+    for col in cols:
+        tot = tot + jnp.exp(col - m_new)
+    m_s[...] = m_new
+    s_s[...] = tot
 
     @pl.when(blk_id == last)
     def _():
@@ -309,10 +307,12 @@
     )(x_top, w_vocab, tgt_rep)
 
 
-GROUP = 4
-SPLIT = 2
+GROUP = 2
+SPLIT = 4
 WID = SHARD // SPLIT
-TOK_BLK = 1024
+TOK_BLK = 2048
+PACE = (6, 8)
+TAKES = ((0, 2, 4, 6), (3, 5, 7, 9), (6, 8, 10, 12), (9, 11, 13, 15))
 
 
 class Reduce:
@@ -419,13 +419,11 @@
     own_v = [pltpu.make_async_copy(shv.at[q], gats[q].slot(HERE), ls.at[q]) for q in range(SPLIT)]
     own_w = [pltpu.make_async_copy(outs[g].own, outs[g].slot(HERE), ls.at[SPLIT + g]) for g in range(n_grp)]
     def slot_of(when):
-        if when >= t_top:
-            when = t_top + (when - t_top) * 5 // SUBL
-        return when if when < t_bwd else t_bwd + (when - t_bwd) // 4
+        return when if when < t_bwd else t_bwd + (when - t_bwd) // 6
 
     per_chunk = n_vocab // SPLIT
     todo = sorted(
-        (per_chunk * (q + 1) + 6 + 9 * n, q, n) for q in range(SPLIT) for n in range(len(gats[q].steps())))
+        (per_chunk * (q + 1) + PACE[0] + PACE[1] * n, q, n) for q in range(SPLIT) for n in range(len(gats[q].steps())))
     acts = [(slot_of(when), gats[q].steps()[n]) for when, q, n in todo]
 
     def emit(j):
@@ -434,11 +432,11 @@
         own_w[j].start()
 
     late = []
-    for j in range(n_grp):
+    for j, when in enumerate(TAKES):
         ops = [functools.partial(reds[j].take, n) for n in range(3)] + [functools.partial(emit, j)]
-        late += [(n, j, op) for n, op in enumerate(ops)]
-        late += [(4 + n, j, op) for n, op in enumerate(outs[j].steps())]
-    late += [(4 * n_grp + n, n_grp, op) for n, op in enumerate(gdb.steps())]
+        late += [(when[n], j, op) for n, op in enumerate(ops)]
+        late += [(when[-1] + 4 * n + 1, j, op) for n, op in enumerate(outs[j].steps())]
+    late += [(TAKES[1][-1] + 4 * n + 3, n_grp, op) for n, op in enumerate(gdb.steps())]
     late = [op for _, _, op in sorted(late, key=lambda item: item[:2])]
 
     @pl.when(step_id == 0)
@@ -463,7 +461,7 @@
         prob = jnp.exp(logits - m_row) * r_row
         ids = lax.broadcasted_iota(jnp.int32, prob.shape, 0) + (place.me * SHARD + q_now * WID)
         dist = ids.astype(F32) - tgt
-        hot = jnp.maximum(1.0 - jnp.maximum(dist, -dist), 0.0)
+        hot = jnp.maximum(1.0 - dist * dist, 0.0)
         acc[...] += mm((prob - hot).astype(BF16), x_val)
 
     for k in range(SPLIT):
@@ -480,19 +478,14 @@
     @pl.when((step_id >= t_top) & (step_id < t_bwd))
     def _():
         blk = wv_ref.shape[1]
-        lane_id = lax.broadcasted_iota(jnp.int32, (LANES, LANES), 1) + (step_id - t_top) * blk
-
-        @pl.loop(0, dx.shape[0] // LANES)
-        def _(part):
-            rs = pl.ds(pl.multiple_of(part * LANES, LANES), LANES)
-            logits = mm(xl_ref[rs, :], wv_ref[...])
-            m_row, r_row = m_ref[rs, :], r_ref[rs, :]
-            off = tgt_ref[rs, :] - lane_id
-            pieces = []
-            for k in range(0, blk, LANES):
-                prob = jnp.exp(logits[:, k:k + LANES] - m_row) * r_row
-                pieces.append(jnp.where(off == k, prob - 1.0, prob).astype(BF16))
-            dx[rs, :] += mm(jnp.concatenate(pieces, axis=1), wv_ref[...], ((1,), (1,)))
+        logits = mm(xl_ref[...], wv_ref[...])
+        m_row, r_row = m_ref[...], r_ref[...]
+        off = tgt_ref[...] - (lax.broadcasted_iota(jnp.int32, m_row.shape, 1) + (step_id - t_top) * blk)
+        pieces = []
+        for k in range(0, blk, LANES):
+            prob = jnp.exp(logits[:, k:k + LANES] - m_row) * r_row
+            pieces.append(jnp.where(off == k, prob - 1.0, prob).astype(BF16))
+        dx[...] += mm(jnp.concatenate(pieces, axis=1), wv_ref[...], ((1,), (1,)))
 
     @pl.when(step_id >= t_bwd)
     def _():
@@ -525,7 +518,7 @@
         pl.when(step_id == t_bwd + GROUP * (j + 1) - 1)(reds[j].start)
 
     done = 0
-    for at, upto in ((4, 1),):
+    for at, upto in ((2, 1), (4, 3), (6, 4)):
         for act in late[done:upto]:
             pl.when(step_id == t_bwd + at)(act)
         done = upto

time: 499 us -> 448 us (0.90)
  Pallas kernels: 456 us -> 404 us
    pallas_call x1, Pallas kernels: 367 us -> 320 us  [run_main(): pl.pallas_call(functools.partial(main_kernel, phases, steps, rows, hid),...]
    pallas_call x1, Pallas kernels: 62.2 us -> 57.1 us  [run_head(): pl.pallas_call(functools.partial(head_kernel, VOCAB_BLK), grid=(VOCAB //...]
where the time goes in v3:
time: 448 us; the launch traced here: 447 us
  Pallas kernels  404 us (90%)
  local copies, waits for them, and re-layouts  39.7 us (9%)
    pallas_call x1, Pallas kernels, run_main(): pl.pallas_call(functools.partial(main_kernel, phases, steps, rows, hid),...  320 us
    pallas_call x1, Pallas kernels, run_head(): pl.pallas_call(functools.partial(head_kernel, VOCAB_BLK), grid=(VOCAB //...  57.1 us
    pallas_call x1, Pallas kernels, run_fwd(): pl.pallas_call(functools.partial(fwd_kernel, steps, rows, hid), grid=(lay...  26.8 us
    slice x1, local copies, waits for them, and re-layouts, local_grads(): return (dw, db, dv[:, :VOCAB], dx_rows)  25 us

profile of v3, /device:TPU:0, one launch (start us, length us, event | category | flops | bytes accessed | tf_op | source)
XLA Modules:
  0.0 446.9 jit_solution(5012989193824556031)
XLA Ops:
  0.6 0.8 broadcast_in_dim.7
  1.4 1.0 constant_dynamic-slice_fusion.1
  2.5 0.8 broadcast_in_dim.8.tgt_ref
  3.3 1.7 copy.9
  5.0 1.2 constant_dynamic-slice_fusion
  6.2 2.2 maximum_select_fusion.wsh_ref
  8.4 26.8 %lstm_fwd.1 = (bf16[8,512,512]{2,1,0:T(8,128)(2,1)}, f32[8,512,1536]{2,1,0:T(8,128)}, bf16[512,256]{1,0:T(8,128)(2,1)}) custom-call(bf16[512,256]{1,0:T(8,128)(2,1)} %bitcast.12, bf16[8,512,1024]{2,1,0:T(8,128)(2,1)} %w_ref.5, f32[8,1024]{1,0:T(8,128)} %b_ref.1), custom_call_target="tpu_custom_call" | custom-call | flops 70000001024 | bytes 40000000 | tf_op jit(solution)/shard_map/lstm_fwd/pallas_call | solution.py:191
  35.2 57.1 %head.1 = (bf16[16384,256]{1,0:T(8,128)(2,1)}, f32[32,8,512]{2,1,0:T(8,128)}, f32[512,128]{1,0:T(8,128)}, f32[512,128]{1,0:T(8,128)}) custom-call(bf16[512,256]{1,0:T(8,128)(2,1)} %get-tuple-element.15.x_ref.xl_ref, bf16[256,32000]{1,0:T(8,128)(2,1)} %wv_ref.1, s32[512,128]{1,0:T(8,128)} %broadcast_in_dim.8.tgt_ref), custom_call_target="tpu_custom_call" | custom-call | flops 10000000000 | bytes 10000000 | tf_op jit(solution)/shard_map/head/pallas_call | solution.py:291
  92.3 320.4 %main.1 = (f32[8,512,1024]{2,1,0:T(8,128)}, f32[8,1024]{1,0:T(8,128)}, f32[512,256]{1,0:T(8,128)}, f32[256,32768]{1,0:T(8,128)}) custom-call(bf16[16384,256]{1,0:T(8,128)(2,1)} %get-tuple-element.16.x_ref, f32[32,8,512]{2,1,0:T(8,128)} %get-tuple-element.17.stat_ref, bf16[256,32000]{1,0:T(8,128)(2,1)} %wv_ref.1, ...), custom_call_target="tpu_custom_call" | custom-call | flops 10000000000 | bytes 10000000 | tf_op jit(solution)/shard_map/main/pallas_call | solution.py:569
  412.8 0.0 slice-start
  412.8 2.3 copy.12
  415.1 0.0 slice-start.1
  415.1 0.0 slice-start.2
  415.1 0.0 slice-start.3
  415.1 25.0 %slice.13 = f32[256,32000]{1,0:T(8,128)} slice(f32[256,32768]{1,0:T(8,128)} %get-tuple-element.24), slice={[0:256], [0:32000]} | slice | bytes 65536000 | tf_op jit(solution)/shard_map/slice | solution.py:627
  440.1 0.0 slice-done
  440.1 0.0 slice-done.1
  440.1 0.0 slice-done.2
  440.1 0.0 slice-done.3
  440.1 0.0 copy-start
  440.2 6.2 %copy.15 = f32[8,512,1024]{2,1,0:T(8,128)} copy(f32[8,512,1024]{2,1,0:T(8,128)S(1)} %bitcast.8) | data formatting | bytes 33554432
  446.3 0.0 copy-done
  446.3 0.6 copy.16
  (1 shorter events, 0.0 us)
Async XLA Ops:
  412.8 27.3 %slice-start = ((s8[16777216]{0:T(1024)(128)(4,1)}), s8[4194304]{0:T(1024)(128)(4,1)S(1)}, s32[]{:S(2)}) async-start(s8[16777216]{0:T(1024)(128)(4,1)} %bitcast.7), calls=%async_computation | async-start | bytes 8388608
  415.1 25.0 %slice-start.1 = ((s8[16777216]{0:T(1024)(128)(4,1)}), s8[4194304]{0:T(1024)(128)(4,1)S(1)}, s32[]{:S(2)}) async-start(s8[16777216]{0:T(1024)(128)(4,1)} %bitcast.7), calls=%async_computation.1 | async-start | bytes 8388608
  415.1 25.0 %slice-start.2 = ((s8[16777216]{0:T(1024)(128)(4,1)}), s8[4194304]{0:T(1024)(128)(4,1)S(1)}, s32[]{:S(2)}) async-start(s8[16777216]{0:T(1024)(128)(4,1)} %bitcast.7), calls=%async_computation.2 | async-start | bytes 8388608
  415.1 25.0 %slice-start.3 = ((s8[16777216]{0:T(1024)(128)(4,1)}), s8[4194304]{0:T(1024)(128)(4,1)S(1)}, s32[]{:S(2)}) async-start(s8[16777216]{0:T(1024)(128)(4,1)} %bitcast.7), calls=%async_computation.3 | async-start | bytes 8388608
  440.1 6.2 %copy-start = (f32[8,1024]{1,0:T(8,128)S(1)}, f32[8,1024]{1,0:T(8,128)}, u32[]{:S(2)}) copy-start(f32[8,1024]{1,0:T(8,128)} %get-tuple-element.31) | copy-start | bytes 98308
